TPU v7x, 32 devices: a whole 2x2x4 slice. The times are simulated.
32 devices in a mesh: gx: 4 (over y, x), gy: 8 (over z, core).
Axes of the slice: x: 2, y: 2, z: 4, core: 2. Of those that a mesh axis runs over, the one named last changes fastest.
Arguments:
- velocity: float32 [2, 2048, 4096], P(None, 'gx', 'gy'), may hold values from -3 to 3
- stress: float32 [3, 2048, 4096], P(None, 'gx', 'gy'), may hold values from -3 to 3
- strength: float32 [2048, 4096], P('gx', 'gy'), may hold values from 0.5 to 4
- ice_mass: float32 [2048, 4096], P('gx', 'gy'), may hold values from 0.3 to 20, as said below
- wind_stress: float32 [2, 2048, 4096], P(None, 'gx', 'gy'), may hold values from -6 to 6
- current: float32 [2, 2048, 4096], P(None, 'gx', 'gy'), may hold values from -3 to 3
- ice_mask: int32 [2048, 4096], P('gx', 'gy'), may hold values from 0 to 1, as said below
- open_water: int32 [2048, 4096], P('gx', 'gy'), may hold values 0 or 1
Outputs:
- new_velocity: float32 [2, 2048, 4096], P(None, 'gx', 'gy')
- new_stress: float32 [3, 2048, 4096], P(None, 'gx', 'gy')
- residual: float32 [], replicated
- kinetic_energy: float32 [], replicated
Inputs may be any that keep to these rules, and one draw needn't show every extreme that they name: `ice_mask`: 1 marks an ocean cell, 0 a land cell. `ice_mass`: positive everywhere.
All inputs are finite; a program needn't handle non-finite values. No bound on the sum of `open_water` on one device may be relied on, other than what follows from the above.
Results may differ from a plain program's by a relative error of at most 0.00002.
Values sent between devices are 32-bit elements; how exact they have to be, the bound alone decides.
A program may use at most 128 MiB of HBM per device.

v0:
```python
import functools

import jax
import jax.numpy as jnp
from jax import lax
from jax.experimental import pallas as pl
from jax.experimental.pallas import tpu as pltpu
from jax.sharding import PartitionSpec as P

ITERS = 4
relax_rate = 0.8
time_step = 0.5
drag_coef = 1.0
coriolis = 0.3
delta_floor = 0.05
MESH = pl.DeviceIdType.MESH

U, V, S1, S2, S12, PR, M, TX, TY, CA, CB = range(11)
NF = 11
PAD = 8
LANE = 128
DIRS = ((-1, 0), (1, 0), (0, -1), (0, 1), (-1, -1), (-1, 1), (1, -1), (1, 1))


def exchange_kernel(
    nx, ny, rows, cols,
    vel, stress, strength, mass, wind, current, mask, water,
    dyn, par,
    strength_v, mass_v, wind_v, current_v, mask_v, water_v,
    pack_l, pack_r, recv_l, recv_r, pack_u, pack_d, recv_u, recv_d,
    load_sem, row_send, row_recv, col_send, col_recv, cor_send, cor_recv,
):
    ix = lax.axis_index("gx")
    iy = lax.axis_index("gy")
    mid = cols - 2 * LANE
    pieces = (
        (0, rows, 0, LANE),
        (0, rows, cols - LANE, LANE),
        (0, 8, LANE, mid),
        (rows - 8, 8, LANE, mid),
        (8, rows - 16, LANE, mid),
    )

    def loads(p):
        r0, nr, c0, nc = pieces[p]
        src = (pl.ds(r0, nr), pl.ds(c0, nc))
        ext = (pl.ds(r0 + PAD, nr), pl.ds(c0, nc))
        both = (slice(None),)
        pairs = (
            (strength.at[src], strength_v.at[src]),
            (mass.at[src], mass_v.at[src]),
            (mask.at[src], mask_v.at[src]),
            (water.at[src], water_v.at[src]),
            (vel.at[both + src], dyn.at[(pl.ds(U, 2),) + ext]),
            (stress.at[both + src], dyn.at[(pl.ds(S1, 3),) + ext]),
            (wind.at[both + src], wind_v.at[both + src]),
            (current.at[both + src], current_v.at[both + src]),
        )
        return [
            pltpu.make_async_copy(a, b, load_sem.at[p * 8 + k])
            for k, (a, b) in enumerate(pairs)
        ]

    for p in range(5):
        for c in loads(p):
            c.start()

    def exists(d):
        return (ix + d[0] >= 0) & (ix + d[0] < nx) & (iy + d[1] >= 0) & (iy + d[1] < ny)

    def peer(d):
        return (ix + d[0], iy + d[1])

    barrier = pltpu.get_barrier_semaphore()
    for d in DIRS:
        @pl.when(exists(d))
        def _():
            pl.semaphore_signal(barrier, inc=1, device_id=peer(d), device_id_type=MESH)
    span = jnp.minimum(ix, 1) + jnp.minimum(nx - 1 - ix, 1) + 1
    breadth = jnp.minimum(iy, 1) + jnp.minimum(ny - 1 - iy, 1) + 1
    pl.semaphore_wait(barrier, span * breadth - 1)

    def prepare(r0, nr, c0, nc, step):
        def body(k, carry):
            r = pl.multiple_of(r0 + k * step, 8)
            src = (pl.ds(r, step), pl.ds(c0, nc))
            dst = (pl.ds(pl.multiple_of(r + PAD, 8), step), pl.ds(c0, nc))
            w = mask_v[src].astype(jnp.float32) * (1.0 - water_v[src].astype(jnp.float32))
            m = mass_v[src]
            inertia = m * (1.0 / time_step)
            diagonal = inertia + drag_coef
            turning = m * coriolis
            scale = (0.25 * w) / (diagonal * diagonal + turning * turning)
            par[(PR - 5,) + dst] = strength_v[src] * w * (relax_rate / (1.0 + relax_rate))
            par[(M - 5,) + dst] = inertia * 4.0
            par[(TX - 5,) + dst] = (wind_v[(0,) + src] + drag_coef * current_v[(0,) + src]) * 4.0
            par[(TY - 5,) + dst] = (wind_v[(1,) + src] + drag_coef * current_v[(1,) + src]) * 4.0
            par[(CA - 5,) + dst] = diagonal * scale
            par[(CB - 5,) + dst] = turning * scale
            return carry

        lax.fori_loop(0, nr // step, body, 0)

    for p in range(4):
        for c in loads(p):
            c.wait()
    prepare(0, rows, 0, LANE, 32)
    prepare(0, rows, cols - LANE, LANE, 32)
    prepare(0, 8, LANE, mid, 8)
    prepare(rows - 8, 8, LANE, mid, 8)

    def plane(f):
        return (dyn, f) if f < 5 else (par, f - 5)

    lane = lax.broadcasted_iota(jnp.int32, (8, LANE), 1)
    half = rows // 2

    def pack(k, carry):
        r = pl.multiple_of(k * 8, 8)
        for out, c0, base in ((pack_l, 0, 0), (pack_r, cols - LANE, 4)):
            acc = jnp.zeros((8, LANE), jnp.float32)
            for h in range(2):
                for f in range(NF):
                    ref, q = plane(f)
                    x = ref[q, pl.ds(pl.multiple_of(r + PAD + h * half, 8), 8), pl.ds(c0, LANE)]
                    at = 4 * f + 64 * h
                    x = pltpu.roll(x, (at + base) % LANE, axis=1) if (at + base) % LANE else x
                    acc = jnp.where((lane >= at) & (lane < at + 4), x, acc)
            out[pl.ds(r, 8), :] = acc
        return carry


    def sends(d):
        dx, dy = d
        k = DIRS.index(d)
        out = []
        if dy == 0:
            src, dst = (pack_u, recv_d) if dx < 0 else (pack_d, recv_u)
            out.append((src, dst, row_send.at[k], row_recv.at[k]))
        else:
            src, dst = (pack_l, recv_r) if dy < 0 else (pack_r, recv_l)
            if dx == 0:
                out.append((src, dst.at[pl.ds(8, half), :], col_send.at[k - 2], col_recv.at[k - 2]))
            else:
                a = 0 if dx < 0 else half - 8
                b = half + 8 if dx < 0 else 0
                out.append((
                    src.at[pl.ds(a, 8), :], dst.at[pl.ds(b, 8), :],
                    cor_send.at[k - 4], cor_recv.at[k - 4],
                ))
        return [
            pltpu.make_async_remote_copy(
                src_ref=a, dst_ref=b, send_sem=s, recv_sem=r,
                device_id=peer(d), device_id_type=MESH,
            )
            for a, b, s, r in out
        ]

    upper = lax.broadcasted_iota(jnp.int32, (8, cols), 0) < 4
    tiles = [(2 * g, min(2 * g + 1, NF - 1)) for g in range((NF + 1) // 2)]

    def edge(f, r):
        ref, q = plane(f)
        return ref[q, r : r + 8, 0:cols]

    for g, (f0, f1) in enumerate(tiles):
        pack_u[g] = jnp.where(upper, edge(f0, PAD), pltpu.roll(edge(f1, PAD), 4, axis=0))
        pack_d[g] = jnp.where(upper, pltpu.roll(edge(f0, rows), 4, axis=0), edge(f1, rows))

    for d in DIRS[:2]:
        @pl.when(exists(d))
        def _():
            for c in sends(d):
                c.start()

    lax.fori_loop(0, half // 8, pack, 0)

    for d in DIRS[2:]:
        @pl.when(exists(d))
        def _():
            for c in sends(d):
                c.start()

    @pl.when(ix == 0)
    def _():
        recv_u[...] = jnp.zeros_like(recv_u)

    @pl.when(ix == nx - 1)
    def _():
        recv_d[...] = jnp.zeros_like(recv_d)

    for dy, buf in ((-1, recv_l), (1, recv_r)):
        @pl.when(~exists((0, dy)))
        def _():
            buf[8 : half + 8, :] = jnp.zeros((half, LANE), jnp.float32)

        for dx, b in ((-1, 0), (1, half + 8)):
            @pl.when(~exists((dx, dy)))
            def _():
                buf[b : b + 8, :] = jnp.zeros((8, LANE), jnp.float32)

    for c in loads(4):
        c.wait()
    prepare(8, rows - 16, LANE, mid, 8)

    for d in DIRS:
        @pl.when(exists(d))
        def _():
            for c in sends((-d[0], -d[1])):
                c.wait_recv()
            for c in sends(d):
                c.wait_send()

    for g, pair in enumerate(tiles):
        top, bottom = recv_u[g], recv_d[g]
        top_turned, bottom_turned = pltpu.roll(top, 4, axis=0), pltpu.roll(bottom, 4, axis=0)
        for j in range(2 if pair[0] < pair[1] else 1):
            ref, q = plane(pair[j])
            ref[q, 0:8, 0:cols] = top if j else top_turned
            ref[q, rows + PAD : rows + 16, 0:cols] = bottom_turned if j else bottom

    def unpack(r, src, h):
        left = recv_l[pl.ds(src, 8), :]
        right = recv_r[pl.ds(src, 8), :]
        for f in range(NF):
            at = 4 * f + 64 * h
            x = pltpu.roll(right, LANE - at, axis=1) if at else right
            y = pltpu.roll(left, (LANE - 4 - at) % LANE, axis=1) if (LANE - 4 - at) % LANE else left
            ref, q = plane(f)
            ref[q, pl.ds(r, 8), pl.ds(cols, LANE)] = jnp.where(
                lane < 4, x, jnp.where(lane >= LANE - 4, y, 0.0)
            )

    unpack(0, 0, 1)
    unpack(rows + PAD, half + 8, 0)

    def body(k, carry):
        s = pl.multiple_of(k * 8 + 8, 8)
        for h in range(2):
            unpack(pl.multiple_of(s + h * half, 8), s, h)
        return carry

    lax.fori_loop(0, half // 8, body, 0)


def roll(x, by, axis):
    return pltpu.roll(x, by % x.shape[axis], axis=axis)


def cycle_kernel(
    rows, cols, dyn, par, new_vel, new_stress, part, vel_a, sig_a, vel_b, sig_b, acc, sem
):
    wide = cols + LANE
    blocks = (rows + 2 * PAD) // 8
    keep = 1.0 / (1.0 + relax_rate)
    sub = lax.broadcasted_iota(jnp.int32, (8, wide), 0)
    first, last = sub == 0, sub == 7
    acc[...] = jnp.zeros_like(acc)

    def at(k):
        return pl.ds(pl.multiple_of(k * 8, 8), 8)

    def sum_diff(vel, k):
        u, v = vel[0, at(k), :], vel[1, at(k), :]
        return u + v, u - v

    def do_stress(vel, sig, to, k, count):
        q, r = sum_diff(vel, jnp.maximum(k - 1, 0))
        q0, r0 = roll(q, 1, 0), roll(r, 1, 0)
        for i in range(count):
            here = at(k + i)
            q, r = sum_diff(vel, k + i)
            q1, r1 = roll(q, 1, 0), roll(r, 1, 0)
            qa, ra = jnp.where(first, q0, q1), jnp.where(first, r0, r1)
            q0, r0 = q1, r1
            x, y = q - ra, r - qa
            z, w = q + ra, r + qa
            d = x + roll(y, 1, 1)
            t = y + roll(x, 1, 1)
            s = z - roll(w, 1, 1)
            e = d * d + 0.25 * (t * t + s * s) + 4.0 * delta_floor * delta_floor
            pr = par[PR - 5, here, :]
            g = pr * lax.rsqrt(e)
            to[0, here, :] = sig[0, here, :] * keep + (g * d - pr)
            to[1, here, :] = sig[1, here, :] * keep + (0.25 * g) * t
            to[2, here, :] = sig[2, here, :] * keep + (0.125 * g) * s

    def normals(sig, k):
        s1, s2, s12 = sig[0, at(k), :], sig[1, at(k), :], sig[2, at(k), :]
        out = s1 + s2, s1 - s2, s12 + s12
        return out, [roll(x, -1, 0) for x in out]

    def do_vel(vel, sig, to, k, count, final):
        now, up = normals(sig, k)
        for i in range(count):
            here = at(k + i)
            later, up_later = normals(sig, jnp.minimum(k + i + 1, blocks - 1))
            n, m, h = now
            nb, mb, hb = (jnp.where(last, b, a) for a, b in zip(up, up_later))
            now, up = later, up_later
            dn, sh, dh, sm = nb - n, hb + h, hb - h, mb + m
            fx = roll(dn + sh, -1, 1) + (dn - sh)
            fy = roll(dh + sm, -1, 1) + (dh - sm)
            u, v = vel[0, here, :], vel[1, here, :]
            mass = par[M - 5, here, :]
            ru = mass * u + (fx + par[TX - 5, here, :])
            rv = mass * v + (fy + par[TY - 5, here, :])
            a, b = par[CA - 5, here, :], par[CB - 5, here, :]
            nu, nv = a * ru + b * rv, a * rv - b * ru
            to[0, here, :] = nu
            to[1, here, :] = nv
            if final:
                du, dv = (nu - u)[:, :cols], (nv - v)[:, :cols]
                acc[2 * i] += du * du + dv * dv
                acc[2 * i + 1] += (mass * (nu * nu + nv * nv))[:, :cols]

    def sweep(old, new, skip, lo, hi, final):
        def body(p, c):
            do_vel(old[0], new[1], new[0], 2 * (p - 2) + skip, 2, final)
            do_stress(old[0], old[1], new[1], 2 * p + skip, 2)
            return c

        lax.fori_loop(lo, hi, body, 0)

    def out_copies(r0, nr, k):
        ext = (slice(None), pl.ds(r0 + PAD, nr), pl.ds(0, cols))
        own = (slice(None), pl.ds(r0, nr))
        return (
            pltpu.make_async_copy(new[0].at[ext], new_vel.at[own], sem.at[2 * k]),
            pltpu.make_async_copy(new[1].at[ext], new_stress.at[own], sem.at[2 * k + 1]),
        )

    start = (dyn.at[0:2], dyn.at[2:5])
    bufs = ((vel_a, sig_a), (vel_b, sig_b))
    pairs = blocks // 2
    for cyc in range(ITERS - 1):
        old = start if cyc == 0 else bufs[(cyc - 1) % 2]
        new = bufs[cyc % 2]
        do_stress(*old, new[1], 0, 4)
        sweep(old, new, 0, 2, pairs, False)
        do_vel(old[0], new[1], new[0], blocks - 4, 4, False)

    old, new = bufs[(ITERS - 2) % 2], bufs[(ITERS - 1) % 2]
    cuts = 4
    per = (blocks - 2) // cuts
    do_stress(*old, new[1], 1, 4)
    for c in range(cuts):
        end = c == cuts - 1
        sweep(old, new, 1, 2 + c * per // 2, pairs - 1 if end else 2 + (c + 1) * per // 2, True)
        if end:
            do_stress(*old, new[1], blocks - 1, 1)
            for j in (5, 3):
                do_vel(old[0], new[1], new[0], blocks - j, 2, True)
        for cp in out_copies(c * per * 8, per * 8, c):
            cp.start()
    part[...] = jnp.zeros_like(part)
    part[0:1, :] = sum_lanes(acc[0] + acc[2], cols)
    part[1:2, :] = sum_lanes(acc[1] + acc[3], cols)
    for c in range(cuts):
        for cp in out_copies(c * per * 8, per * 8, c):
            cp.wait()


def sum_lanes(x, cols):
    t = x[:, 0:LANE]
    for c in range(LANE, cols, LANE):
        t = t + x[:, c : c + LANE]
    return jnp.sum(t, axis=0, keepdims=True)


def sum_kernel(nx, ny, scale, part, out, slots, send_sem, recv_sem):
    n = nx * ny
    me = lax.axis_index("gx") * ny + lax.axis_index("gy")

    def target(k):
        t = lax.rem(me + k, n)
        return (t // ny, lax.rem(t, ny))

    barrier = pltpu.get_barrier_semaphore()

    def greet(k, c):
        pl.semaphore_signal(barrier, inc=1, device_id=target(k), device_id_type=MESH)
        return c

    lax.fori_loop(1, n, greet, 0)
    pl.semaphore_wait(barrier, n - 1)

    def copy(k):
        return pltpu.make_async_remote_copy(
            src_ref=part, dst_ref=slots.at[me], send_sem=send_sem.at[k], recv_sem=recv_sem.at[k],
            device_id=target(k), device_id_type=MESH,
        )

    def start(k, c):
        copy(k).start()
        return c

    lax.fori_loop(1, n, start, 0)
    slots[pl.ds(me, 1)] = part[...][None]

    def wait(k, c):
        copy(k).wait()
        return c

    lax.fori_loop(1, n, wait, 0)
    total = jnp.sum(slots[...], axis=0)
    total = jnp.sum(total, axis=1, keepdims=True)
    out[...] = jnp.broadcast_to(total * scale, out.shape)


def per_device(nx, ny, velocity, stress, strength, ice_mass, wind, current, ice_mask, open_water):
    _, rows, cols = velocity.shape
    wide, tall, half = cols + LANE, rows + 2 * PAD, rows // 2
    f32, i32 = jnp.float32, jnp.int32
    hbm = pl.BlockSpec(memory_space=pl.ANY)
    vmem = pl.BlockSpec(memory_space=pltpu.VMEM)
    dma = pltpu.SemaphoreType.DMA
    dyn, par = pl.pallas_call(
        functools.partial(exchange_kernel, nx, ny, rows, cols),
        out_shape=(
            pltpu.VMEM((5, tall, wide), f32),
            pltpu.VMEM((6, tall, wide), f32),
        ),
        in_specs=[pl.BlockSpec(memory_space=pltpu.HBM)] * 8,
        out_specs=(vmem, vmem),
        scratch_shapes=[
            pltpu.VMEM((rows, cols), f32),
            pltpu.VMEM((rows, cols), f32),
            pltpu.VMEM((2, rows, cols), f32),
            pltpu.VMEM((2, rows, cols), f32),
            pltpu.VMEM((rows, cols), i32),
            pltpu.VMEM((rows, cols), i32),
            pltpu.VMEM((half, LANE), f32),
            pltpu.VMEM((half, LANE), f32),
            pltpu.VMEM((half + 16, LANE), f32),
            pltpu.VMEM((half + 16, LANE), f32),
            pltpu.VMEM(((NF + 1) // 2, 8, cols), f32),
            pltpu.VMEM(((NF + 1) // 2, 8, cols), f32),
            pltpu.VMEM(((NF + 1) // 2, 8, cols), f32),
            pltpu.VMEM(((NF + 1) // 2, 8, cols), f32),
            dma((40,)), dma((2,)), dma((2,)), dma((2,)), dma((2,)), dma((4,)), dma((4,)),
        ],
        compiler_params=pltpu.CompilerParams(
            collective_id=0, has_side_effects=True, vmem_limit_bytes=K1_VMEM
        ),
        name="exchange",
    )(
        *[
            pltpu.with_memory_space_constraint(x, pltpu.HBM)
            for x in (velocity, stress, strength, ice_mass, wind, current, ice_mask, open_water)
        ]
    )
    new_vel, new_stress, part = pl.pallas_call(
        functools.partial(cycle_kernel, rows, cols),
        out_shape=(
            jax.ShapeDtypeStruct(velocity.shape, f32),
            jax.ShapeDtypeStruct(stress.shape, f32),
            jax.ShapeDtypeStruct((8, LANE), f32),
        ),
        in_specs=[vmem, vmem],
        out_specs=(hbm, hbm, vmem),
        scratch_shapes=[
            pltpu.VMEM((2, tall, wide), f32),
            pltpu.VMEM((3, tall, wide), f32),
            pltpu.VMEM((2, tall, wide), f32),
            pltpu.VMEM((3, tall, wide), f32),
            pltpu.VMEM((4, 8, cols), f32),
            dma((8,)),
        ],
        compiler_params=pltpu.CompilerParams(vmem_limit_bytes=K2_VMEM),
        name="subcycles",
    )(dyn, par)
    sums = pl.pallas_call(
        functools.partial(sum_kernel, nx, ny, 1.0 / (rows * nx * cols * ny)),
        out_shape=jax.ShapeDtypeStruct((8, LANE), f32),
        in_specs=[vmem],
        out_specs=vmem,
        scratch_shapes=[
            pltpu.VMEM((nx * ny, 8, LANE), f32),
            dma((nx * ny,)),
            dma((nx * ny,)),
        ],
        compiler_params=pltpu.CompilerParams(
            collective_id=1, has_side_effects=True, vmem_limit_bytes=4 << 20
        ),
        name="totals",
    )(part)
    return new_vel, new_stress, sums[0, 0], sums[1, 0] * 0.0625


K1_VMEM = 12 << 20
K2_VMEM = 24 << 20


def solution(mesh):
    two, three = P("gx", "gy"), P(None, "gx", "gy")
    return jax.shard_map(
        functools.partial(per_device, mesh.shape["gx"], mesh.shape["gy"]),
        mesh=mesh,
        in_specs=(three, three, two, two, three, three, two, two),
        out_specs=(three, three, P(), P()),
        check_vma=False,
    )
```

profile of v0, /device:TPU:0, one launch (start us, length us, event | category | flops | bytes accessed | tf_op | source)
XLA Modules:
  0.0 52.9 jit_solution(10055857166761725105)
XLA Ops:
  0.6 15.6 %exchange.1 = (f32[5,528,640]{2,1,0:T(8,128)S(1)}, f32[6,528,640]{2,1,0:T(8,128)S(1)}) custom-call(f32[2,512,512]{2,1,0:T(8,128)} %vel.1, f32[3,512,512]{2,1,0:T(8,128)} %stress.1, f32[512,512]{1,0:T(8,128)} %strength.1, f32[512,512]{1,0:T(8,128)} %mass.1, f32[2,512,512]{2,1,0:T(8,128)} %wind.1, f32[2,512,512]{2,1,0:T(8,128)} %current.1, s32[512,512]{1,0:T(8,128)} %mask.1, ...), custom_call_target="tpu_custom_call" | custom-call | tf_op jit(solution)/shard_map/exchange/pallas_call | solution.py:418
  16.3 21.9 %subcycles.1 = (f32[2,512,512]{2,1,0:T(8,128)}, f32[3,512,512]{2,1,0:T(8,128)}, f32[8,128]{1,0:T(8,128)S(1)}) custom-call(f32[5,528,640]{2,1,0:T(8,128)S(1)} %get-tuple-element.9.dyn, f32[6,528,640]{2,1,0:T(8,128)S(1)} %get-tuple-element.10.par), custom_call_target="tpu_custom_call" | custom-call | tf_op jit(solution)/shard_map/subcycles/pallas_call | solution.py:453
  38.1 12.5 %totals.1 = f32[8,128]{1,0:T(8,128)S(1)} custom-call(f32[8,128]{1,0:T(8,128)S(1)} %get-tuple-element.13.part), custom_call_target="tpu_custom_call" | custom-call | tf_op jit(solution)/shard_map/totals/pallas_call | solution.py:473
  50.6 0.5 fusion
where the time goes:
time: 53.1 us; the launch traced here: 52.9 us
  Pallas kernels  49.9 us (94%)
  between operations  2.43 us (5%)
    pallas_call x1, Pallas kernels, per_device(): pl.pallas_call(functools.partial(cycle_kernel, rows, cols), out_shape=(ja...  21.9 us
    pallas_call x1, Pallas kernels, per_device(): pl.pallas_call(functools.partial(exchange_kernel, nx, ny, rows, cols), ou...  15.6 us
    pallas_call x1, Pallas kernels, per_device(): pl.pallas_call(functools.partial(sum_kernel, nx, ny, 1.0 / (rows * nx * c...  12.5 us

commit v1 on v0

v1 whole, which is shorter than its diff:
```python
import functools

import jax
import jax.numpy as jnp
from jax import lax
from jax.experimental import pallas as pl
from jax.experimental.pallas import tpu as pltpu
from jax.sharding import PartitionSpec as P

ITERS = 4
relax_rate = 0.8
time_step = 0.5
drag_coef = 1.0
coriolis = 0.3
delta_floor = 0.05
MESH = pl.DeviceIdType.MESH

Q, R, QX, RX, AL, BE, S2 = range(7)
PR, M, TQ, TR, CA, CB = range(6)
SENT = ((0, Q), (0, R), (0, AL), (0, BE), (0, S2)) + tuple((1, f) for f in range(6))
NF = len(SENT)
PAIRS = (NF + 1) // 2
LANE = 128
PAD = 8
UN = 4
DIRS = ((-1, 0), (1, 0), (0, -1), (0, 1), (-1, -1), (-1, 1), (1, -1), (1, 1))
CORNERS = ((-1, 0), (1, 0)) + DIRS[4:]
f32 = jnp.float32


def iota(axis):
    return lax.broadcasted_iota(jnp.int32, (8, LANE), axis)


def roll(x, by, axis):
    by %= x.shape[axis]
    return pltpu.roll(x, by, axis=axis) if by else x


def here(k):
    return pl.ds(pl.multiple_of(k * 8 + PAD, 8), 8)


def near(k, off):
    return pl.ds(k * 8 + PAD + off, 8)


def shift(xs, by, first, last):
    n = len(xs)
    turned = [roll(x, by, 1) for x in xs]
    if by > 0:
        return [jnp.where(first, turned[(j - 1) % n], turned[j]) for j in range(n)]
    return [jnp.where(last, turned[(j + 1) % n], turned[j]) for j in range(n)]


class Sweep:
    def __init__(self, tiles, turned):
        self.n, self.turned = tiles, turned
        self.first, self.last = iota(1) == 0, iota(1) == LANE - 1

    def spread(self, st, k):
        for f in (Q, R):
            xs = shift([st[f, j, here(k), :] for j in range(self.n)], 1, self.first, self.last)
            for j, x in enumerate(xs):
                st[f + 2, j, here(k), :] = x

    def stress(self, old, new, par, k):
        at, up = here(k), near(k, -1)
        keep = 1.0 / (1.0 + relax_rate)
        for j in range(self.n):
            q, r, qx, rx = (old[f, j, at, :] for f in (Q, R, QX, RX))
            qa, ra, qxa, rxa = (old[f, j, up, :] for f in (Q, R, QX, RX))
            a, b = q - qxa, rx - ra
            if self.turned:
                d, s = a - b, a + b
                t = (r - rxa) - (qx - qa)
            else:
                d, s = a + b, a - b
                t = (r - rxa) + (qx - qa)
            e = (d * d + 4.0 * delta_floor * delta_floor) + 0.25 * (t * t + s * s)
            pr = par[PR, j, at, :]
            g = pr * lax.rsqrt(e)
            h = 0.25 * g
            push, side = g * d - pr, h * s
            new[AL, j, at, :] = old[AL, j, at, :] * keep + (push + side)
            new[BE, j, at, :] = old[BE, j, at, :] * keep + (push - side)
            new[S2, j, at, :] = old[S2, j, at, :] * keep + h * t

    def force(self, new, frc, k):
        at, dn = here(k), near(k, 1)
        a, c = [], []
        for j in range(self.n):
            ad, s, sd, b = new[AL, j, dn, :], new[S2, j, at, :], new[S2, j, dn, :], new[BE, j, at, :]
            if self.turned:
                a.append(ad + s)
                c.append(sd + b)
            else:
                a.append(ad - s)
                c.append(sd - b)
        for f, xs in ((0, a), (1, c)):
            for j, x in enumerate(shift(xs, -1, self.first, self.last)):
                frc[f, j, at, :] = x

    def velocity(self, old, new, frc, par, k, acc=None):
        at, dn = here(k), near(k, 1)
        out = []
        for j in range(self.n):
            al, s, sd, bd = new[AL, j, at, :], new[S2, j, at, :], new[S2, j, dn, :], new[BE, j, dn, :]
            fa, fc = frc[0, j, at, :], frc[1, j, at, :]
            if self.turned:
                fq, fr = fa - (sd + al), fc - (bd + s)
            else:
                fq, fr = fa + (sd - al), fc + (bd - s)
            q, r, m = old[Q, j, at, :], old[R, j, at, :], par[M, j, at, :]
            x = m * q + (fq + par[TQ, j, at, :])
            y = m * r + (fr + par[TR, j, at, :])
            ca, cb = par[CA, j, at, :], par[CB, j, at, :]
            nq, nr = ca * x - cb * y, ca * y + cb * x
            new[Q, j, at, :] = nq
            new[R, j, at, :] = nr
            out.append((nq, nr))
            if acc is not None:
                dq, dr = nq - q, nr - r
                acc(j, dq * dq + dr * dr, m * (nq * nq + nr * nr))
        if acc is None:
            for f in (0, 1):
                xs = shift([o[f] for o in out], 1, self.first, self.last)
                for j, x in enumerate(xs):
                    new[f + 2, j, at, :] = x


def main_sweep(sw, old, new, frc, par, blocks, final):
    n = sw.n
    trips = blocks // UN
    zero = jnp.zeros((8, LANE), f32)
    sums = (zero,) * (2 * n)

    def vel(ks, sums):
        sums = list(sums)

        def acc(j, x, y):
            sums[2 * j] += x
            sums[2 * j + 1] += y

        for k in ks:
            if not final:
                sw.velocity(old, new, frc, par, k)
            elif not isinstance(k, int) or 0 < k < blocks - 1:
                sw.velocity(old, new, frc, par, k, acc)
        return tuple(sums)

    for k in range(UN):
        sw.stress(old, new, par, k)
    for k in range(UN - 1):
        sw.force(new, frc, k)
    for k in range(UN, 2 * UN):
        sw.stress(old, new, par, k)
    sums = vel(range(UN - 1), sums)
    for k in range(UN - 1, 2 * UN - 1):
        sw.force(new, frc, k)
    for k in range(2 * UN, 3 * UN):
        sw.stress(old, new, par, k)

    def body(p, sums):
        sums = vel([UN * (p - 2) - 1 + i for i in range(UN)], sums)
        for i in range(UN):
            sw.force(new, frc, UN * (p - 1) - 1 + i)
        for i in range(UN):
            sw.stress(old, new, par, UN * p + i)
        return sums

    sums = lax.fori_loop(3, trips, body, sums)
    sums = vel([blocks - UN - 1 - UN + i for i in range(UN)], sums)
    for i in range(UN + 1):
        sw.force(new, frc, blocks - UN - 1 + i)
    return vel([blocks - UN - 1 + i for i in range(UN + 1)], sums)


def core_kernel(
    nx, ny, rows, cols,
    vel, stress, strength, mass, wind, current, mask, water,
    vel_out, stress_out, total_out,
    strength_v, mass_v, mask_v, water_v, vel_v, stress_v, wind_v, current_v,
    st_a, st_b, frc, par,
    pack_u, pack_d, recv_u, recv_d, own_l, own_r, recv_l, recv_r,
    corner_u, corner_d, corner_in,
    row_a, row_b, row_f, row_p, col_a, col_b, col_f, col_p,
    packed, edge_t, edge, mine, slots,
    load_sem, send_sem, recv_sem, sum_send, sum_recv,
):
    ix = lax.axis_index("gx")
    iy = lax.axis_index("gy")
    n, tall, blocks = cols // LANE, rows // LANE, rows // 8
    chunks = 8
    per = rows // chunks
    lane, sub = iota(1), iota(0)
    zero = jnp.zeros((8, LANE), f32)

    def loads(c):
        part = pl.ds(c * per, per)
        both = slice(None)
        pairs = (
            (strength.at[part], strength_v.at[part]),
            (mass.at[part], mass_v.at[part]),
            (mask.at[part], mask_v.at[part]),
            (water.at[part], water_v.at[part]),
            (vel.at[both, part], vel_v.at[both, part]),
            (stress.at[both, part], stress_v.at[both, part]),
            (wind.at[both, part], wind_v.at[both, part]),
            (current.at[both, part], current_v.at[both, part]),
        )
        return [pltpu.make_async_copy(a, b, load_sem.at[c, k]) for k, (a, b) in enumerate(pairs)]

    for c in [0, chunks - 1] + list(range(1, chunks - 1)):
        for cp in loads(c):
            cp.start()

    count = nx * ny
    me = ix * ny + iy

    def target(k):
        t = lax.rem(me + k, count)
        return (t // ny, lax.rem(t, ny))

    barrier = pltpu.get_barrier_semaphore()

    def greet(k, c):
        pl.semaphore_signal(barrier, inc=1, device_id=target(k), device_id_type=MESH)
        return c

    lax.fori_loop(1, count, greet, 0)

    for st in (st_a, st_b):
        for f in range(7):
            for j in range(n):
                st[f, j, 0:8, :] = zero
                st[f, j, rows + PAD : rows + 16, :] = zero
    for st in (row_a, row_b, col_a, col_b):
        for side in range(2):
            for f in range(7):
                for j in range(st.shape[2]):
                    st[side, f, j, 0:8, :] = zero
                    st[side, f, j, 24:32, :] = zero

    sw = Sweep(n, False)

    def prepare(k):
        rowsl = pl.ds(pl.multiple_of(k * 8, 8), 8)
        at = here(k)
        qs, rs = [], []
        ends = []
        for j in range(n):
            src = (rowsl, slice(j * LANE, (j + 1) * LANE))
            w = mask_v[src].astype(f32) * (1.0 - water_v[src].astype(f32))
            m = mass_v[src]
            inertia = m * (1.0 / time_step)
            diagonal = inertia + drag_coef
            turning = m * coriolis
            scale = (0.5 * w) / (diagonal * diagonal + turning * turning)
            tx = wind_v[(0,) + src] + drag_coef * current_v[(0,) + src]
            ty = wind_v[(1,) + src] + drag_coef * current_v[(1,) + src]
            u, v = vel_v[(0,) + src], vel_v[(1,) + src]
            s1, s2, s12 = (stress_v[(i,) + src] for i in range(3))
            t = s12 + s12
            q, r = u + v, u - v
            state = {Q: q, R: r, AL: s1 + t, BE: s1 - t, S2: s2}
            fixed = {
                PR: strength_v[src] * w * (relax_rate / (1.0 + relax_rate)),
                M: inertia * 2.0,
                TQ: (tx + ty) * 2.0,
                TR: (tx - ty) * 2.0,
                CA: diagonal * scale,
                CB: turning * scale,
            }
            for f, x in state.items():
                st_a[f, j, at, :] = x
            for f, x in fixed.items():
                par[f, j, at, :] = x
            qs.append(q)
            rs.append(r)
            if j in (0, n - 1):
                ends.append([(state, fixed)[a][f] for a, f in SENT])
        for f, xs in ((QX, qs), (RX, rs)):
            for j, x in enumerate(shift(xs, 1, sw.first, sw.last)):
                st_a[f, j, at, :] = x
        low, high = ends[0], ends[-1]
        packs = [zero, zero]
        for i in range(NF):
            x = roll(jnp.where(lane < LANE // 2, low[i], high[i]), 16 * (i % 8) + 8, 1)
            g = lane // 16 == i % 8
            packs[i // 8] = jnp.where(g, x, packs[i // 8])
        for i in range(2):
            packed[i, rowsl, :] = packs[i]

    def prepare_chunk(c):
        for cp in loads(c):
            cp.wait()

        def body(k, carry):
            prepare(k)
            return carry

        lax.fori_loop(c * (per // 8), (c + 1) * (per // 8), body, 0)

    def exists(d):
        return (ix + d[0] >= 0) & (ix + d[0] < nx) & (iy + d[1] >= 0) & (iy + d[1] < ny)

    def message(d, which):
        k = DIRS.index(d)
        dx, dy = d
        out = []
        if which == 1:
            pass
        elif dy == 0:
            out.append((pack_u, recv_d, k) if dx < 0 else (pack_d, recv_u, k))
        elif dx == 0:
            out.append((own_l, recv_r, k) if dy < 0 else (own_r, recv_l, k))
        if dx and which != 0:
            c = CORNERS.index(d)
            back = CORNERS.index((-dx, -dy))
            out.append((corner_u if dx < 0 else corner_d, corner_in.at[back], 4 + c))
        return [
            pltpu.make_async_remote_copy(
                src_ref=a, dst_ref=b, send_sem=send_sem.at[s], recv_sem=recv_sem.at[s],
                device_id=(ix + dx, iy + dy), device_id_type=MESH,
            )
            for a, b, s in out
        ]

    def plane(i):
        a, f = SENT[i]
        return (st_a, par)[a], f

    prepare_chunk(0)
    prepare_chunk(chunks - 1)
    top, bottom = slice(PAD, PAD + 8), slice(rows, rows + 8)
    for g in range(PAIRS):
        i0, i1 = 2 * g, min(2 * g + 1, NF - 1)
        (a0, f0), (a1, f1) = plane(i0), plane(i1)
        for j in range(n):
            pack_u[g, j] = jnp.where(sub < 4, a0[f0, j, top, :], roll(a1[f1, j, top, :], 4, 0))
            pack_d[g, j] = jnp.where(sub < 4, roll(a0[f0, j, bottom, :], 4, 0), a1[f1, j, bottom, :])
    pl.semaphore_wait(barrier, count - 1)
    for d in DIRS[:2]:
        @pl.when(exists(d))
        def _():
            message(d, 0)[0].start()

    for c in range(1, chunks - 1):
        prepare_chunk(c)

    for i in range(2):
        for t in range(tall):
            x = packed[i, t * LANE : (t + 1) * LANE, :].T
            for f in range(8 * i, min(8 * i + 8, NF)):
                o = 16 * (f - 8 * i)
                own_r[f, t] = x[o : o + 8]
                own_l[f, t] = x[o + 8 : o + 16]
                a, g = SENT[f]
                dst = (col_a, col_p)[a]
                dst[0, g, t, 16:24, :] = x[o + 8 : o + 16]
                dst[1, g, t, 8:16, :] = x[o : o + 8]
    up, down = zero, zero
    for i in range(2 * NF):
        src = own_l if i < NF else own_r
        g = lane // 4 == i
        up = jnp.where(g, roll(src[i % NF, 0], 4 * i, 1), up)
        down = jnp.where(g, roll(src[i % NF, tall - 1], 4 * i + 4, 1), down)
    corner_u[...] = up
    corner_d[...] = down
    for d in DIRS[2:4]:
        @pl.when(exists(d))
        def _():
            message(d, 0)[0].start()
    for d in CORNERS:
        @pl.when(exists(d))
        def _():
            message(d, 1)[0].start()

    for i in range(NF):
        a, f = SENT[i]
        src, g = plane(i)
        dst = (row_a, row_p)[a]
        for j in range(n):
            x, y = (roll(src[g, j, b * 8 + PAD : b * 8 + PAD + 8, :], 4, 0) for b in (0, 1))
            dst[0, f, j, 8:16, :] = x
            dst[0, f, j, 16:24, :] = jnp.where(sub < 4, x, y)
            x, y = (roll(src[g, j, b * 8 + PAD : b * 8 + PAD + 8, :], 4, 0) for b in (blocks - 2, blocks - 1))
            dst[1, f, j, 8:16, :] = jnp.where(sub < 4, x, y)
            dst[1, f, j, 16:24, :] = y

    main_sweep(sw, st_a, st_b, frc, par, blocks, False)
    main_sweep(sw, st_b, st_a, frc, par, blocks, False)

    def clear(ref, lead):
        for i in lead:
            ref[i] = jnp.zeros(ref.shape[1:], f32)

    for d, buf in (((-1, 0), recv_u), ((1, 0), recv_d), ((0, -1), recv_l), ((0, 1), recv_r)):
        @pl.when(~exists(d))
        def _():
            clear(buf, range(buf.shape[0]))

    for c, d in enumerate(CORNERS):
        @pl.when(~exists(d))
        def _():
            corner_in[c] = zero

    for d in DIRS:
        @pl.when(exists(d))
        def _():
            for cp in message((-d[0], -d[1]), 2):
                cp.wait_recv()
            for cp in message(d, 2):
                cp.wait_send()

    for i in range(NF):
        a, f = SENT[i]
        dst = (row_a, row_p)[a]
        g, odd = divmod(i, 2)
        for j in range(n):
            x, y = recv_u[g, j], recv_d[g, j]
            x = roll(x, 4, 0) if odd else x
            y = y if odd else roll(y, 4, 0)
            dst[0, f, j, 8:16, :] = jnp.where(sub < 4, x, dst[0, f, j, 8:16, :])
            dst[1, f, j, 16:24, :] = jnp.where(sub < 4, dst[1, f, j, 16:24, :], y)
        dst = (col_a, col_p)[a]
        for t in range(tall):
            dst[0, f, t, 8:16, :] = recv_l[i, t]
            dst[1, f, t, 16:24, :] = recv_r[i, t]

        def corner(u, d, at):
            x = roll(corner_in[CORNERS.index(u)], LANE - 4 - 4 * at, 1)
            y = roll(corner_in[CORNERS.index(d)], -4 * at, 1)
            return jnp.where(lane < 4, y, jnp.where(lane >= LANE - 4, x, 0.0))

        dst[0, f, tall, 8:16, :] = corner((-1, -1), (1, -1), NF + i)
        dst[0, f, tall, 16:24, :] = corner((-1, 0), (1, 0), i)
        dst[1, f, tall, 8:16, :] = corner((-1, 0), (1, 0), NF + i)
        dst[1, f, tall, 16:24, :] = corner((-1, 1), (1, 1), i)

    strips = [
        (s, a.at[side], b.at[side], fr.at[side], p.at[side], side)
        for s, a, b, fr, p in (
            (sw, row_a, row_b, row_f, row_p),
            (Sweep(tall + 1, True), col_a, col_b, col_f, col_p),
        )
        for side in range(2)
    ]
    for s, a, b, fr, p, _ in strips:
        for k in range(2):
            s.spread(a, k)
    sums = [[zero, zero] for _ in range(n)]
    more = [zero, zero]
    for cyc in range(ITERS):
        final = cyc == ITERS - 1
        flip = cyc % 2
        for s, a, b, fr, p, _ in strips:
            old, new = (b, a) if flip else (a, b)
            for k in range(2):
                s.stress(old, new, p, k)
        for s, a, b, fr, p, _ in strips:
            new = a if flip else b
            for k in range(2):
                s.force(new, fr, k)
        for s, a, b, fr, p, side in strips:
            old, new = (b, a) if flip else (a, b)
            for k in range(2):
                if not final:
                    s.velocity(old, new, fr, p, k)
                    continue

                def acc(j, x, y):
                    if s.turned and (j == tall or k == side):
                        return
                    good = sub >= 4 if (k == 0) else sub < 4
                    box = more if s.turned else sums[j]
                    box[0] += jnp.where(good, x, 0.0)
                    box[1] += jnp.where(good, y, 0.0)

                s.velocity(old, new, fr, p, k, acc)
    row_e, col_e = (row_a, col_a) if ITERS % 2 == 0 else (row_b, col_b)

    main_sweep(sw, st_a, st_b, frc, par, blocks, False)
    inner = main_sweep(sw, st_b, st_a, frc, par, blocks, True)

    for j in range(n):
        good = lane >= 4 if j == 0 else lane < LANE - 4 if j == n - 1 else None
        if n == 1:
            good = (lane >= 4) & (lane < LANE - 4)
        for i in range(2):
            x = inner[2 * j + i] + sums[j][i]
            more[i] += x if good is None else jnp.where(good, x, 0.0)
    x, y = (jnp.sum(m, axis=0, keepdims=True) for m in more)
    x, y = x + roll(x, LANE // 2, 1), y + roll(y, LANE // 2, 1)
    half = lax.broadcasted_iota(jnp.int32, (1, LANE), 1) < LANE // 2
    part = jnp.where(half, x, y)
    mine[...] = part

    def sum_copy(k):
        return pltpu.make_async_remote_copy(
            src_ref=mine, dst_ref=slots.at[me], send_sem=sum_send.at[k], recv_sem=sum_recv.at[k],
            device_id=target(k), device_id_type=MESH,
        )

    def start(k, c):
        sum_copy(k).start()
        return c

    lax.fori_loop(1, count, start, 0)
    slots[pl.ds(me, 1)] = part[None]

    for t in range(tall):
        for o, f in enumerate((Q, R, AL, BE, S2)):
            x = jnp.where(sub < 4, col_e[0, f, t, 16:24, :], col_e[1, f, t, 8:16, :])
            edge_t[o * 8 : o * 8 + 8, :] = roll(x, 4, 0)
        edge[t * LANE : (t + 1) * LANE, :] = edge_t[...].T

    def emit(k, row, src, at):
        rowsl = pl.ds(row, 8)
        ev = edge[rowsl, :]
        es = [roll(ev, LANE - 4 - 8 * o, 1) for o in range(5)]
        for j in range(n):
            vals = [src[f, j, at, :] for f in (Q, R, AL, BE, S2)]
            if j == 0:
                vals = [jnp.where(lane < 4, e, x) for e, x in zip(es, vals)]
            if j == n - 1:
                vals = [jnp.where(lane >= LANE - 4, e, x) for e, x in zip(es, vals)]
            q, r, al, be, s2 = vals
            c = slice(j * LANE, (j + 1) * LANE)
            vel_out[0, rowsl, c] = 0.5 * (q + r)
            vel_out[1, rowsl, c] = 0.5 * (q - r)
            stress_out[0, rowsl, c] = 0.5 * (al + be)
            stress_out[1, rowsl, c] = s2
            stress_out[2, rowsl, c] = 0.25 * (al - be)

    emit(0, 0, row_e.at[0], slice(12, 20))
    emit(blocks - 1, rows - 8, row_e.at[1], slice(12, 20))

    def body(k, c):
        emit(k, pl.multiple_of(k * 8, 8), st_a, here(k))
        return c

    lax.fori_loop(1, blocks - 1, body, 0)

    def wait(k, c):
        sum_copy(k).wait()
        return c

    lax.fori_loop(1, count, wait, 0)
    total = slots[0]
    for i in range(1, count):
        total = total + slots[i]
    scale = 1.0 / (rows * nx * cols * ny)
    x = jnp.sum(jnp.where(half, total, 0.0), axis=1, keepdims=True) * (0.5 * scale)
    y = jnp.sum(jnp.where(half, 0.0, total), axis=1, keepdims=True) * (0.0625 * scale)
    total_out[...] = jnp.where(half, x, y)


def write_kernel(vel, stress, new_vel, new_stress, sem):
    copies = [
        pltpu.make_async_copy(vel, new_vel, sem.at[0]),
        pltpu.make_async_copy(stress, new_stress, sem.at[1]),
    ]
    for c in copies:
        c.start()
    for c in copies:
        c.wait()


def per_device(nx, ny, velocity, stress, strength, ice_mass, wind, current, ice_mask, open_water):
    _, rows, cols = velocity.shape
    n, tall, strip = cols // LANE, rows // LANE, rows + 2 * PAD
    i32 = jnp.int32
    vmem = pl.BlockSpec(memory_space=pltpu.VMEM)
    hbm = pl.BlockSpec(memory_space=pl.ANY)
    dma = pltpu.SemaphoreType.DMA
    V = pltpu.VMEM
    count = nx * ny
    new_vel, new_stress, total = pl.pallas_call(
        functools.partial(core_kernel, nx, ny, rows, cols),
        out_shape=(V((2, rows, cols), f32), V((3, rows, cols), f32), V((1, LANE), f32)),
        in_specs=[pl.BlockSpec(memory_space=pltpu.HBM)] * 8,
        out_specs=(vmem, vmem, vmem),
        scratch_shapes=[
            V((rows, cols), f32), V((rows, cols), f32), V((rows, cols), i32), V((rows, cols), i32),
            V((2, rows, cols), f32), V((3, rows, cols), f32), V((2, rows, cols), f32), V((2, rows, cols), f32),
            V((7, n, strip, LANE), f32), V((7, n, strip, LANE), f32),
            V((2, n, strip, LANE), f32), V((6, n, strip, LANE), f32),
            V((PAIRS, n, 8, LANE), f32), V((PAIRS, n, 8, LANE), f32),
            V((PAIRS, n, 8, LANE), f32), V((PAIRS, n, 8, LANE), f32),
            V((NF, tall, 8, LANE), f32), V((NF, tall, 8, LANE), f32),
            V((NF, tall, 8, LANE), f32), V((NF, tall, 8, LANE), f32),
            V((8, LANE), f32), V((8, LANE), f32), V((6, 8, LANE), f32),
            V((2, 7, n, 32, LANE), f32), V((2, 7, n, 32, LANE), f32),
            V((2, 2, n, 32, LANE), f32), V((2, 6, n, 32, LANE), f32),
            V((2, 7, tall + 1, 32, LANE), f32), V((2, 7, tall + 1, 32, LANE), f32),
            V((2, 2, tall + 1, 32, LANE), f32), V((2, 6, tall + 1, 32, LANE), f32),
            V((2, rows, LANE), f32), V((LANE, LANE), f32), V((rows, LANE), f32),
            V((1, LANE), f32), V((count, 1, LANE), f32),
            dma((8, 8)), dma((10,)), dma((10,)), dma((count,)), dma((count,)),
        ],
        compiler_params=pltpu.CompilerParams(
            collective_id=0, has_side_effects=True, vmem_limit_bytes=48 << 20
        ),
        name="core",
    )(
        *[
            pltpu.with_memory_space_constraint(x, pltpu.HBM)
            for x in (velocity, stress, strength, ice_mass, wind, current, ice_mask, open_water)
        ]
    )
    new_vel, new_stress = pl.pallas_call(
        write_kernel,
        out_shape=(
            jax.ShapeDtypeStruct(velocity.shape, f32),
            jax.ShapeDtypeStruct(stress.shape, f32),
        ),
        in_specs=[vmem, vmem],
        out_specs=(hbm, hbm),
        scratch_shapes=[dma((2,))],
        compiler_params=pltpu.CompilerParams(vmem_limit_bytes=8 << 20),
        name="write",
    )(new_vel, new_stress)
    return new_vel, new_stress, total[0, 0], total[0, LANE - 1]


def solution(mesh):
    two, three = P("gx", "gy"), P(None, "gx", "gy")
    return jax.shard_map(
        functools.partial(per_device, mesh.shape["gx"], mesh.shape["gy"]),
        mesh=mesh,
        in_specs=(three, three, two, two, three, three, two, two),
        out_specs=(three, three, P(), P()),
        check_vma=False,
    )
```

time: 53.1 us -> 42.5 us (0.80)
  Pallas kernels: 49.9 us -> 41.1 us
  between operations: 2.43 us -> 0.65 us
    pallas_call x3 -> x2, Pallas kernels: 49.9 us -> 41.1 us  [the longest x1 38.8 us: per_device(): pl.pallas_call(functools.partial(core_kernel, nx, ny, rows, cols), out_sh...]
where the time goes in v1:
time: 42.5 us; the launch traced here: 42.4 us
  Pallas kernels  41.1 us (97%)
  between operations  0.65 us (2%)
  local copies, waits for them, and re-layouts  0.58 us (1%)
    pallas_call x1, Pallas kernels, per_device(): pl.pallas_call(functools.partial(core_kernel, nx, ny, rows, cols), out_sh...  38.8 us
    pallas_call x1, Pallas kernels, per_device(): pl.pallas_call(write_kernel, out_shape=(jax.ShapeDtypeStruct(velocity.sha...  2.37 us

profile of v1, /device:TPU:0, one launch (start us, length us, event | category | flops | bytes accessed | tf_op | source)
XLA Modules:
  0.0 42.4 jit_solution(9499776358896116562)
XLA Ops:
  0.6 38.8 %core.1 = (f32[2,512,512]{2,1,0:T(8,128)S(1)}, f32[3,512,512]{2,1,0:T(8,128)S(1)}, f32[1,128]{1,0:T(1,128)S(1)}) custom-call(f32[2,512,512]{2,1,0:T(8,128)} %vel.1, f32[3,512,512]{2,1,0:T(8,128)} %stress.1, f32[512,512]{1,0:T(8,128)} %strength.1, f32[512,512]{1,0:T(8,128)} %mass.1, f32[2,512,512]{2,1,0:T(8,128)} %wind.1, f32[2,512,512]{2,1,0:T(8,128)} %current.1, ...), custom_call_target="tpu_custom_call" | custom-call | tf_op jit(solution)/shard_map/core/pallas_call | solution.py:580
  39.4 2.4 %write.1 = (f32[2,512,512]{2,1,0:T(8,128)}, f32[3,512,512]{2,1,0:T(8,128)}) custom-call(f32[2,512,512]{2,1,0:T(8,128)S(1)} %get-tuple-element.9.vel, f32[3,512,512]{2,1,0:T(8,128)S(1)} %get-tuple-element.10.stress), custom_call_target="tpu_custom_call" | custom-call | tf_op jit(solution)/shard_map/write/pallas_call | solution.py:613
  41.8 0.6 %fusion = (f32[1,1]{1,0:T(1,128)}, f32[1,1]{1,0:T(1,128)}) fusion(f32[1,128]{1,0:T(1,128)S(1)} %get-tuple-element.13), kind=kLoop, calls=%fused_computation | loop fusion | bytes 16 | tf_op jit(solution)/shard_map/slice | solution.py:625

commit v2 on v1

v2 whole, which is shorter than its diff:
```python
import functools

import jax
import jax.numpy as jnp
from jax import lax
from jax.experimental import pallas as pl
from jax.experimental.pallas import tpu as pltpu
from jax.sharding import PartitionSpec as P

ITERS = 4
relax_rate = 0.8
time_step = 0.5
drag_coef = 1.0
coriolis = 0.3
delta_floor = 0.05
MESH = pl.DeviceIdType.MESH

Q, R = range(2)
AL, BE, S2 = range(3)
PR, M, TQ, TR, CA, CB = range(6)
SENT = ((0, Q), (0, R), (1, AL), (1, BE), (1, S2)) + tuple((2, f) for f in range(6))
NF = len(SENT)
PAIRS = (NF + 1) // 2
LANE = 128
PAD = 8
FRONT = 128
UN = 4
DIRS = ((-1, 0), (1, 0), (0, -1), (0, 1), (-1, -1), (-1, 1), (1, -1), (1, 1))
CORNERS = ((-1, 0), (1, 0)) + DIRS[4:]
f32 = jnp.float32


def iota(axis):
    return lax.broadcasted_iota(jnp.int32, (8, LANE), axis)


def roll(x, by, axis):
    by %= x.shape[axis]
    return pltpu.roll(x, by, axis=axis) if by else x


def rows8(row):
    if isinstance(row, int):
        return slice(row, row + 8)
    base, off = row
    return pl.ds(base + off if off % 8 else pl.multiple_of(base + off, 8), 8)


def select(mask, x, y):
    return lax.select(mask, x, y)


def shift(xs, by, first, last):
    n = len(xs)
    turned = [roll(x, by, 1) for x in xs]
    if by > 0:
        return [select(first, turned[(j - 1) % n], turned[j]) for j in range(n)]
    return [select(last, turned[(j + 1) % n], turned[j]) for j in range(n)]


class View:
    def __init__(self, ref, pad=PAD, base=None):
        self.ref, self.pad, self.base = ref, pad, base

    def at(self, i, off=0):
        row = self.pad + 8 * i + off
        return rows8(row if self.base is None else (self.base, row))

    def load(self, f, j, i, off=0):
        return self.ref[f, j, self.at(i, off), :]

    def store(self, f, j, i, x):
        self.ref[f, j, self.at(i), :] = x


class Sweep:
    def __init__(self, tiles, turned):
        self.n, self.turned = tiles, turned
        self.first, self.last = iota(1) == 0, iota(1) == LANE - 1

    def spread(self, ve, vx, i):
        for f in (Q, R):
            xs = shift([ve.load(f, j, i) for j in range(self.n)], 1, self.first, self.last)
            for j, x in enumerate(xs):
                vx.store(f, j, i, x)

    def stress(self, ve, vx, old, new, par, i):
        keep = 1.0 / (1.0 + relax_rate)
        for j in range(self.n):
            q, r, qx, rx = (v.load(f, j, i) for v in (ve, vx) for f in (Q, R))
            qa, ra, qxa, rxa = (v.load(f, j, i, -1) for v in (ve, vx) for f in (Q, R))
            a, b = q - qxa, rx - ra
            if self.turned:
                d, s = a - b, a + b
                t = (r - rxa) - (qx - qa)
            else:
                d, s = a + b, a - b
                t = (r - rxa) + (qx - qa)
            e = (d * d + 4.0 * delta_floor * delta_floor) + 0.25 * (t * t + s * s)
            pr = par.load(PR, j, i)
            g = pr * lax.rsqrt(e)
            h = 0.25 * g
            push, side = g * d - pr, h * s
            new.store(AL, j, i, old.load(AL, j, i) * keep + (push + side))
            new.store(BE, j, i, old.load(BE, j, i) * keep + (push - side))
            new.store(S2, j, i, old.load(S2, j, i) * keep + h * t)

    def force(self, ss, frc, i):
        a, c = [], []
        for j in range(self.n):
            ad, s, sd, b = ss.load(AL, j, i, 1), ss.load(S2, j, i), ss.load(S2, j, i, 1), ss.load(BE, j, i)
            if self.turned:
                a.append(ad + s)
                c.append(sd + b)
            else:
                a.append(ad - s)
                c.append(sd - b)
        for f, xs in ((0, a), (1, c)):
            for j, x in enumerate(shift(xs, -1, self.first, self.last)):
                frc.store(f, j, i, x)

    def velocity(self, old, new, ss, frc, par, i):
        for j in range(self.n):
            al, s, sd, bd = ss.load(AL, j, i), ss.load(S2, j, i), ss.load(S2, j, i, 1), ss.load(BE, j, i, 1)
            fa, fc = frc.load(0, j, i), frc.load(1, j, i)
            if self.turned:
                fq, fr = fa - (sd + al), fc - (bd + s)
            else:
                fq, fr = fa + (sd - al), fc + (bd - s)
            q, r, m = old.load(Q, j, i), old.load(R, j, i), par.load(M, j, i)
            x = m * q + (fq + par.load(TQ, j, i))
            y = m * r + (fr + par.load(TR, j, i))
            ca, cb = par.load(CA, j, i), par.load(CB, j, i)
            new.store(Q, j, i, ca * x - cb * y)
            new.store(R, j, i, ca * y + cb * x)

    def reduce(self, old, new, par, i, add):
        for j in range(self.n):
            nq, nr = new.load(Q, j, i), new.load(R, j, i)
            dq, dr = nq - old.load(Q, j, i), nr - old.load(R, j, i)
            add(j, dq * dq + dr * dr, par.load(M, j, i) * (nq * nq + nr * nr))


class Stream:
    def __init__(self, sw, ve, vx, ss, frc, par, rows):
        self.sw, self.ve, self.vx, self.ss, self.frc, self.par, self.rows = sw, ve, vx, ss, frc, par, rows

    def base(self, p, lag, mod):
        x = p * (8 * UN) - 8 * UN * lag
        return pl.multiple_of(lax.rem(x + (lag * mod if lag else 0), mod), 8 * UN)

    def step(self, p, stages):
        sw, rows, unit = self.sw, self.rows, 8 * UN
        row = pl.multiple_of(p * unit, unit)
        ss = [View(self.ss, PAD, self.base(p, lag, rows)) for lag in (0, 2, 3)]
        par = [View(self.par, PAD, self.base(p, lag, rows)) for lag in (0, 3)]
        slots = [View(self.frc, PAD, pl.multiple_of(lax.rem(p + k, 2) * unit, unit)) for k in (0, 1)]
        was = lambda lag: View(self.ve, FRONT - lag * unit, row)
        now = lambda lag: View(self.ve, FRONT + rows - lag * unit, row)
        vx = View(self.vx, PAD, self.base(p, 0, 2 * rows))
        shifted = View(self.vx, PAD, pl.multiple_of(lax.rem(row + 3 * rows - 4 * unit, 2 * rows), unit))
        todo = {
            "velocity": (was(3), now(3), ss[2], slots[1], par[1]),
            "force": (ss[1], slots[0]),
            "stress": (was(0), vx, ss[0], ss[0], par[0]),
            "spread": (now(4), shifted),
        }
        for name in stages:
            for i in range(UN):
                getattr(sw, name)(*todo[name], i)

    def run(self):
        steps = ITERS * self.rows // (8 * UN)
        every = ("velocity", "force", "stress", "spread")
        parts = (
            (0, 2, every[2:3]), (2, 3, every[1:3]), (3, 4, every[:3]),
            (4, steps, every), (steps, steps + 3, every[:2]),
        )
        for lo, hi, stages in parts:
            def body(p, carry):
                self.step(p, stages)
                return carry

            lax.fori_loop(lo, hi, body, 0)


def core_kernel(
    nx, ny, rows, cols,
    vel, stress, strength, mass, wind, current, mask, water,
    vel_out, stress_out, total_out,
    strength_v, mass_v, mask_v, water_v, vel_v, stress_v, wind_v, current_v,
    ve, vx, ss, frc, par, acc,
    pack_u, pack_d, recv_u, recv_d, own_l, own_r, recv_l, recv_r,
    corner_u, corner_d, corner_in,
    row_va, row_vb, row_sa, row_sb, row_x, row_f, row_p, col_va, col_vb, col_sa, col_sb, col_x, col_f, col_p,
    packed, edge_t, edge, mine, slots,
    load_sem, send_sem, recv_sem, sum_send, sum_recv,
):
    ix = lax.axis_index("gx")
    iy = lax.axis_index("gy")
    n, tall, blocks = cols // LANE, rows // LANE, rows // 8
    chunks = 8
    per = rows // chunks
    lane, sub = iota(1), iota(0)
    zero = jnp.zeros((8, LANE), f32)

    def loads(c):
        part = pl.ds(c * per, per)
        both = slice(None)
        pairs = (
            (strength.at[part], strength_v.at[part]),
            (mass.at[part], mass_v.at[part]),
            (mask.at[part], mask_v.at[part]),
            (water.at[part], water_v.at[part]),
            (vel.at[both, part], vel_v.at[both, part]),
            (stress.at[both, part], stress_v.at[both, part]),
            (wind.at[both, part], wind_v.at[both, part]),
            (current.at[both, part], current_v.at[both, part]),
        )
        return [pltpu.make_async_copy(a, b, load_sem.at[c, k]) for k, (a, b) in enumerate(pairs)]

    for c in [0, chunks - 1] + list(range(1, chunks - 1)):
        for cp in loads(c):
            cp.start()

    count = nx * ny
    me = ix * ny + iy

    def target(k):
        t = lax.rem(me + k, count)
        return (t // ny, lax.rem(t, ny))

    barrier = pltpu.get_barrier_semaphore()

    def greet(k, c):
        pl.semaphore_signal(barrier, inc=1, device_id=target(k), device_id_type=MESH)
        return c

    lax.fori_loop(1, count, greet, 0)

    for j in range(n):
        for f in range(2):
            ve[f, j, FRONT - 8 : FRONT, :] = zero
            vx[f, j, 0:8, :] = zero
        for f in range(3):
            ss[f, j, rows + PAD : rows + 16, :] = zero
    for st in (row_va, row_vb, row_sa, row_sb, row_x, col_va, col_vb, col_sa, col_sb, col_x):
        for side in range(2):
            for f in range(st.shape[1]):
                for j in range(st.shape[2]):
                    st[side, f, j, 0:8, :] = zero
                    st[side, f, j, 24:32, :] = zero

    sw = Sweep(n, False)

    def prepare(base, i):
        rowsl, at = rows8((base, 8 * i)), rows8((base, 8 * i + PAD))
        first = rows8((base, 8 * i + FRONT))
        ends = []
        for j in range(n):
            src = (rowsl, slice(j * LANE, (j + 1) * LANE))
            w = mask_v[src].astype(f32) * (1.0 - water_v[src].astype(f32))
            m = mass_v[src]
            inertia = m * (1.0 / time_step)
            diagonal = inertia + drag_coef
            turning = m * coriolis
            scale = (0.5 * w) / (diagonal * diagonal + turning * turning)
            tx = wind_v[(0,) + src] + drag_coef * current_v[(0,) + src]
            ty = wind_v[(1,) + src] + drag_coef * current_v[(1,) + src]
            u, v = vel_v[(0,) + src], vel_v[(1,) + src]
            s1, s2, s12 = (stress_v[(i,) + src] for i in range(3))
            t = s12 + s12
            q, r = u + v, u - v
            moving = {Q: q, R: r}
            state = {AL: s1 + t, BE: s1 - t, S2: s2}
            fixed = {
                PR: strength_v[src] * w * (relax_rate / (1.0 + relax_rate)),
                M: inertia * 2.0,
                TQ: (tx + ty) * 2.0,
                TR: (tx - ty) * 2.0,
                CA: diagonal * scale,
                CB: turning * scale,
            }
            for f, x in moving.items():
                ve[f, j, first, :] = x
            for f, x in state.items():
                ss[f, j, at, :] = x
            for f, x in fixed.items():
                par[f, j, at, :] = x
            if j in (0, n - 1):
                ends.append([(moving, state, fixed)[a][f] for a, f in SENT])
        low, high = ends[0], ends[-1]
        packs = [zero, zero]
        for i in range(NF):
            x = roll(select(lane < LANE // 2, low[i], high[i]), 16 * (i % 8) + 8, 1)
            g = (lane >= 16 * (i % 8)) & (lane < 16 * (i % 8) + 16)
            packs[i // 8] = select(g, x, packs[i // 8])
        for i in range(2):
            packed[i, rowsl, :] = packs[i]

    def prepare_chunk(c):
        for cp in loads(c):
            cp.wait()

        group = min(UN, per // 8)

        def body(p, carry):
            base = pl.multiple_of(p * (8 * group), 8 * group)
            for i in range(group):
                prepare(base, i)
            for i in range(group):
                sw.spread(View(ve, FRONT, base), View(vx, PAD, base), i)
            return carry

        lax.fori_loop(c * (per // 8) // group, (c + 1) * (per // 8) // group, body, 0)

    def exists(d):
        return (ix + d[0] >= 0) & (ix + d[0] < nx) & (iy + d[1] >= 0) & (iy + d[1] < ny)

    def message(d, which):
        k = DIRS.index(d)
        dx, dy = d
        out = []
        if which == 1:
            pass
        elif dy == 0:
            out.append((pack_u, recv_d, k) if dx < 0 else (pack_d, recv_u, k))
        elif dx == 0:
            out.append((own_l, recv_r, k) if dy < 0 else (own_r, recv_l, k))
        if dx and which != 0:
            c = CORNERS.index(d)
            back = CORNERS.index((-dx, -dy))
            out.append((corner_u if dx < 0 else corner_d, corner_in.at[back], 4 + c))
        return [
            pltpu.make_async_remote_copy(
                src_ref=a, dst_ref=b, send_sem=send_sem.at[s], recv_sem=recv_sem.at[s],
                device_id=(ix + dx, iy + dy), device_id_type=MESH,
            )
            for a, b, s in out
        ]

    def plane(i, j, block):
        a, f = SENT[i]
        row = block * 8 + (FRONT, PAD, PAD)[a]
        return (ve, ss, par)[a][f, j, row : row + 8, :]

    prepare_chunk(0)
    prepare_chunk(chunks - 1)
    for g in range(PAIRS):
        i0, i1 = 2 * g, min(2 * g + 1, NF - 1)
        for j in range(n):
            pack_u[g, j] = select(sub < 4, plane(i0, j, 0), roll(plane(i1, j, 0), 4, 0))
            pack_d[g, j] = select(sub < 4, roll(plane(i0, j, blocks - 1), 4, 0), plane(i1, j, blocks - 1))
    pl.semaphore_wait(barrier, count - 1)
    for d in DIRS[:2]:
        @pl.when(exists(d))
        def _():
            message(d, 0)[0].start()

    for c in range(1, chunks - 1):
        prepare_chunk(c)

    for i in range(2):
        for t in range(tall):
            x = packed[i, t * LANE : (t + 1) * LANE, :].T
            for f in range(8 * i, min(8 * i + 8, NF)):
                o = 16 * (f - 8 * i)
                own_r[f, t] = x[o : o + 8]
                own_l[f, t] = x[o + 8 : o + 16]
                a, g = SENT[f]
                dst = (col_va, col_sa, col_p)[a]
                dst[0, g, t, 16:24, :] = x[o + 8 : o + 16]
                dst[1, g, t, 8:16, :] = x[o : o + 8]
    up, down = zero, zero
    for i in range(2 * NF):
        src = own_l if i < NF else own_r
        g = (lane >= 4 * i) & (lane < 4 * i + 4)
        up = select(g, roll(src[i % NF, 0], 4 * i, 1), up)
        down = select(g, roll(src[i % NF, tall - 1], 4 * i + 4, 1), down)
    corner_u[...] = up
    corner_d[...] = down
    for d in DIRS[2:4]:
        @pl.when(exists(d))
        def _():
            message(d, 0)[0].start()
    for d in CORNERS:
        @pl.when(exists(d))
        def _():
            message(d, 1)[0].start()

    for i in range(NF):
        a, f = SENT[i]
        dst = (row_va, row_sa, row_p)[a]
        for j in range(n):
            x, y = (roll(plane(i, j, b), 4, 0) for b in (0, 1))
            dst[0, f, j, 8:16, :] = x
            dst[0, f, j, 16:24, :] = select(sub < 4, x, y)
            x, y = (roll(plane(i, j, b), 4, 0) for b in (blocks - 2, blocks - 1))
            dst[1, f, j, 8:16, :] = select(sub < 4, x, y)
            dst[1, f, j, 16:24, :] = y

    Stream(sw, ve, vx, ss, frc, par, rows).run()

    def clear(ref, lead):
        for i in lead:
            ref[i] = jnp.zeros(ref.shape[1:], f32)

    for d, buf in (((-1, 0), recv_u), ((1, 0), recv_d), ((0, -1), recv_l), ((0, 1), recv_r)):
        @pl.when(~exists(d))
        def _():
            clear(buf, range(buf.shape[0]))

    for c, d in enumerate(CORNERS):
        @pl.when(~exists(d))
        def _():
            corner_in[c] = zero

    for d in DIRS:
        @pl.when(exists(d))
        def _():
            for cp in message((-d[0], -d[1]), 2):
                cp.wait_recv()
            for cp in message(d, 2):
                cp.wait_send()

    for i in range(NF):
        a, f = SENT[i]
        dst = (row_va, row_sa, row_p)[a]
        g, odd = divmod(i, 2)
        for j in range(n):
            x, y = recv_u[g, j], recv_d[g, j]
            x = roll(x, 4, 0) if odd else x
            y = y if odd else roll(y, 4, 0)
            dst[0, f, j, 8:16, :] = select(sub < 4, x, dst[0, f, j, 8:16, :])
            dst[1, f, j, 16:24, :] = select(sub < 4, dst[1, f, j, 16:24, :], y)
        dst = (col_va, col_sa, col_p)[a]
        for t in range(tall):
            dst[0, f, t, 8:16, :] = recv_l[i, t]
            dst[1, f, t, 16:24, :] = recv_r[i, t]

        def corner(u, d, at):
            x = roll(corner_in[CORNERS.index(u)], LANE - 4 - 4 * at, 1)
            y = roll(corner_in[CORNERS.index(d)], -4 * at, 1)
            return select(lane < 4, y, select(lane >= LANE - 4, x, zero))

        dst[0, f, tall, 8:16, :] = corner((-1, -1), (1, -1), NF + i)
        dst[0, f, tall, 16:24, :] = corner((-1, 0), (1, 0), i)
        dst[1, f, tall, 8:16, :] = corner((-1, 0), (1, 0), NF + i)
        dst[1, f, tall, 16:24, :] = corner((-1, 1), (1, 1), i)

    strips = []
    for s, va, vb, sa, sb, x, fr, p in (
        (sw, row_va, row_vb, row_sa, row_sb, row_x, row_f, row_p),
        (Sweep(tall + 1, True), col_va, col_vb, col_sa, col_sb, col_x, col_f, col_p),
    ):
        for i in range(2):
            strips.append((s, i, *(View(y.at[i]) for y in (va, vb, sa, sb, x, fr, p))))

    def strip_cycles(t, carry):
        for flip in (False, True):
            for s, i, va, vb, sa, sb, x, fr, p in strips:
                for k in range(2):
                    s.spread(vb if flip else va, x, k)
            for s, i, va, vb, sa, sb, x, fr, p in strips:
                for k in range(2):
                    s.stress(vb if flip else va, x, *((sb, sa) if flip else (sa, sb)), p, k)
            for s, i, va, vb, sa, sb, x, fr, p in strips:
                for k in range(2):
                    s.force(sa if flip else sb, fr, k)
            for s, i, va, vb, sa, sb, x, fr, p in strips:
                for k in range(2):
                    s.velocity(*((vb, va, sa) if flip else (va, vb, sb)), fr, p, k)
        return carry

    lax.fori_loop(0, ITERS // 2, strip_cycles, 0)
    row_e, col_e = (row_va, row_sa), (col_va, col_sa)
    sums = [[zero, zero] for _ in range(n)]
    more = [zero, zero]
    for s, i, va, vb, sa, sb, x, fr, p in strips:
        for k in range(2):
            def add(j, x, y):
                if s.turned and (j == tall or k == i):
                    return
                good = sub >= 4 if k == 0 else sub < 4
                box = more if s.turned else sums[j]
                box[0] += select(good, x, zero)
                box[1] += select(good, y, zero)

            s.reduce(vb, va, p, k, add)

    last = FRONT + ITERS * rows
    acc[...] = jnp.zeros_like(acc)

    def reduce_rows(p, group, lead):
        part = {}

        def add(j, x, y):
            for i, z in ((2 * j, x), (2 * j + 1, y)):
                part[i] = part[i] + z if i in part else z

        base = pl.multiple_of(p * (8 * group), 8 * group)
        for i in range(group):
            sw.reduce(View(ve, last - rows + lead, base), View(ve, last + lead, base), View(par, PAD + lead, base), i, add)
        for i, z in part.items():
            acc[i] += z

    group = 2
    lax.fori_loop(0, (blocks - 2) // group, lambda p, c: (reduce_rows(p, group, 8), c)[1], 0)

    for j in range(n):
        good = lane >= 4 if j == 0 else lane < LANE - 4 if j == n - 1 else None
        if n == 1:
            good = (lane >= 4) & (lane < LANE - 4)
        for i in range(2):
            x = acc[2 * j + i] + sums[j][i]
            more[i] += x if good is None else jnp.where(good, x, 0.0)
    x, y = (jnp.sum(m, axis=0, keepdims=True) for m in more)
    x, y = x + roll(x, LANE // 2, 1), y + roll(y, LANE // 2, 1)
    half = lax.broadcasted_iota(jnp.int32, (1, LANE), 1) < LANE // 2
    part = jnp.where(half, x, y)
    mine[...] = part

    def sum_copy(k):
        return pltpu.make_async_remote_copy(
            src_ref=mine, dst_ref=slots.at[me], send_sem=sum_send.at[k], recv_sem=sum_recv.at[k],
            device_id=target(k), device_id_type=MESH,
        )

    def start(k, c):
        sum_copy(k).start()
        return c

    lax.fori_loop(1, count, start, 0)
    slots[pl.ds(me, 1)] = part[None]

    for t in range(tall):
        for o, (a, f) in enumerate(SENT[:5]):
            x = select(sub < 4, col_e[a][0, f, t, 16:24, :], col_e[a][1, f, t, 8:16, :])
            edge_t[o * 8 : o * 8 + 8, :] = roll(x, 4, 0)
        edge[t * LANE : (t + 1) * LANE, :] = edge_t[...].T

    def emit(rowsl, src):
        ev = edge[rowsl, :]
        es = [roll(ev, LANE - 4 - 8 * o, 1) for o in range(5)]
        for j in range(n):
            vals = [src[a][0][f, j, src[a][1], :] for a, f in SENT[:5]]
            if j == 0:
                vals = [select(lane < 4, e, x) for e, x in zip(es, vals)]
            if j == n - 1:
                vals = [select(lane >= LANE - 4, e, x) for e, x in zip(es, vals)]
            q, r, al, be, s2 = vals
            c = slice(j * LANE, (j + 1) * LANE)
            vel_out[0, rowsl, c] = 0.5 * (q + r)
            vel_out[1, rowsl, c] = 0.5 * (q - r)
            stress_out[0, rowsl, c] = 0.5 * (al + be)
            stress_out[1, rowsl, c] = s2
            stress_out[2, rowsl, c] = 0.25 * (al - be)

    def row_strip(i):
        return [(x.at[i], slice(12, 20)) for x in row_e]

    emit(slice(0, 8), row_strip(0))
    emit(slice(rows - 8, rows), row_strip(1))
    batch = 6 if (blocks - 2) % 6 == 0 else 2

    def body(p, c):
        base = pl.multiple_of(p * (8 * batch), 8)
        for i in range(1, batch + 1):
            src = [(ve, rows8((base, 8 * i + last))), (ss, rows8((base, 8 * i + PAD)))]
            emit(rows8((base, 8 * i)), src)
        return c

    lax.fori_loop(0, (blocks - 2) // batch, body, 0)

    def wait(k, c):
        sum_copy(k).wait()
        return c

    lax.fori_loop(1, count, wait, 0)
    total = slots[0]
    for i in range(1, count):
        total = total + slots[i]
    scale = 1.0 / (rows * nx * cols * ny)
    x = jnp.sum(jnp.where(half, total, 0.0), axis=1, keepdims=True) * (0.5 * scale)
    y = jnp.sum(jnp.where(half, 0.0, total), axis=1, keepdims=True) * (0.0625 * scale)
    total_out[...] = jnp.where(half, x, y)


def write_kernel(vel, stress, new_vel, new_stress, sem):
    copies = [
        pltpu.make_async_copy(vel, new_vel, sem.at[0]),
        pltpu.make_async_copy(stress, new_stress, sem.at[1]),
    ]
    for c in copies:
        c.start()
    for c in copies:
        c.wait()


def per_device(nx, ny, velocity, stress, strength, ice_mass, wind, current, ice_mask, open_water):
    _, rows, cols = velocity.shape
    n, tall, strip = cols // LANE, rows // LANE, rows + 2 * PAD
    i32 = jnp.int32
    vmem = pl.BlockSpec(memory_space=pltpu.VMEM)
    hbm = pl.BlockSpec(memory_space=pl.ANY)
    dma = pltpu.SemaphoreType.DMA
    V = pltpu.VMEM
    count = nx * ny
    new_vel, new_stress, total = pl.pallas_call(
        functools.partial(core_kernel, nx, ny, rows, cols),
        out_shape=(V((2, rows, cols), f32), V((3, rows, cols), f32), V((1, LANE), f32)),
        in_specs=[pl.BlockSpec(memory_space=pltpu.HBM)] * 8,
        out_specs=(vmem, vmem, vmem),
        scratch_shapes=[
            V((rows, cols), f32), V((rows, cols), f32), V((rows, cols), i32), V((rows, cols), i32),
            V((2, rows, cols), f32), V((3, rows, cols), f32), V((2, rows, cols), f32), V((2, rows, cols), f32),
            V((2, n, FRONT + (ITERS + 1) * rows, LANE), f32), V((2, n, 2 * rows + PAD, LANE), f32),
            V((3, n, strip, LANE), f32), V((2, n, 2 * 8 * UN + PAD, LANE), f32),
            V((6, n, strip, LANE), f32), V((2 * n, 8, LANE), f32),
            V((PAIRS, n, 8, LANE), f32), V((PAIRS, n, 8, LANE), f32),
            V((PAIRS, n, 8, LANE), f32), V((PAIRS, n, 8, LANE), f32),
            V((NF, tall, 8, LANE), f32), V((NF, tall, 8, LANE), f32),
            V((NF, tall, 8, LANE), f32), V((NF, tall, 8, LANE), f32),
            V((8, LANE), f32), V((8, LANE), f32), V((6, 8, LANE), f32),
            V((2, 2, n, 32, LANE), f32), V((2, 2, n, 32, LANE), f32),
            V((2, 3, n, 32, LANE), f32), V((2, 3, n, 32, LANE), f32), V((2, 2, n, 32, LANE), f32),
            V((2, 2, n, 32, LANE), f32), V((2, 6, n, 32, LANE), f32),
            V((2, 2, tall + 1, 32, LANE), f32), V((2, 2, tall + 1, 32, LANE), f32),
            V((2, 3, tall + 1, 32, LANE), f32), V((2, 3, tall + 1, 32, LANE), f32), V((2, 2, tall + 1, 32, LANE), f32),
            V((2, 2, tall + 1, 32, LANE), f32), V((2, 6, tall + 1, 32, LANE), f32),
            V((2, rows, LANE), f32), V((LANE, LANE), f32), V((rows, LANE), f32),
            V((1, LANE), f32), V((count, 1, LANE), f32),
            dma((8, 8)), dma((10,)), dma((10,)), dma((count,)), dma((count,)),
        ],
        compiler_params=pltpu.CompilerParams(
            collective_id=0, has_side_effects=True, vmem_limit_bytes=48 << 20
        ),
        name="core",
    )(
        *[
            pltpu.with_memory_space_constraint(x, pltpu.HBM)
            for x in (velocity, stress, strength, ice_mass, wind, current, ice_mask, open_water)
        ]
    )
    new_vel, new_stress = pl.pallas_call(
        write_kernel,
        out_shape=(
            jax.ShapeDtypeStruct(velocity.shape, f32),
            jax.ShapeDtypeStruct(stress.shape, f32),
        ),
        in_specs=[vmem, vmem],
        out_specs=(hbm, hbm),
        scratch_shapes=[dma((2,))],
        compiler_params=pltpu.CompilerParams(vmem_limit_bytes=8 << 20),
        name="write",
    )(new_vel, new_stress)
    return new_vel, new_stress, total[0, 0], total[0, LANE - 1]


def solution(mesh):
    two, three = P("gx", "gy"), P(None, "gx", "gy")
    return jax.shard_map(
        functools.partial(per_device, mesh.shape["gx"], mesh.shape["gy"]),
        mesh=mesh,
        in_specs=(three, three, two, two, three, three, two, two),
        out_specs=(three, three, P(), P()),
        check_vma=False,
    )
```

time: 42.5 us -> 35.8 us (0.84)
  Pallas kernels: 41.1 us -> 34.4 us
    pallas_call x1, Pallas kernels: 38.8 us -> 32.1 us  [per_device(): pl.pallas_call(functools.partial(core_kernel, nx, ny, rows, cols), out_sh...]
where the time goes in v2:
time: 35.8 us; the launch traced here: 35.7 us
  Pallas kernels  34.4 us (96%)
  between operations  0.65 us (2%)
  local copies, waits for them, and re-layouts  0.58 us (2%)
    pallas_call x1, Pallas kernels, per_device(): pl.pallas_call(functools.partial(core_kernel, nx, ny, rows, cols), out_sh...  32.1 us
    pallas_call x1, Pallas kernels, per_device(): pl.pallas_call(write_kernel, out_shape=(jax.ShapeDtypeStruct(velocity.sha...  2.37 us

profile of v2, /device:TPU:0, one launch (start us, length us, event | category | flops | bytes accessed | tf_op | source)
XLA Modules:
  0.0 35.7 jit_solution(15509893271545987376)
XLA Ops:
  0.6 32.1 %core.1 = (f32[2,512,512]{2,1,0:T(8,128)S(1)}, f32[3,512,512]{2,1,0:T(8,128)S(1)}, f32[1,128]{1,0:T(1,128)S(1)}) custom-call(f32[2,512,512]{2,1,0:T(8,128)} %vel.1, f32[3,512,512]{2,1,0:T(8,128)} %stress.1, f32[512,512]{1,0:T(8,128)} %strength.1, f32[512,512]{1,0:T(8,128)} %mass.1, f32[2,512,512]{2,1,0:T(8,128)} %wind.1, f32[2,512,512]{2,1,0:T(8,128)} %current.1, ...), custom_call_target="tpu_custom_call" | custom-call | tf_op jit(solution)/shard_map/core/pallas_call | solution.py:609
  32.7 2.4 %write.1 = (f32[2,512,512]{2,1,0:T(8,128)}, f32[3,512,512]{2,1,0:T(8,128)}) custom-call(f32[2,512,512]{2,1,0:T(8,128)S(1)} %get-tuple-element.9.vel, f32[3,512,512]{2,1,0:T(8,128)S(1)} %get-tuple-element.10.stress), custom_call_target="tpu_custom_call" | custom-call | tf_op jit(solution)/shard_map/write/pallas_call | solution.py:645
  35.1 0.6 %fusion = (f32[1,1]{1,0:T(1,128)}, f32[1,1]{1,0:T(1,128)}) fusion(f32[1,128]{1,0:T(1,128)S(1)} %get-tuple-element.13), kind=kLoop, calls=%fused_computation | loop fusion | bytes 16 | tf_op jit(solution)/shard_map/slice | solution.py:657

commit v3 on v2

--- a/solution.py
+++ b/solution.py
@@ -16,7 +16,7 @@
 MESH = pl.DeviceIdType.MESH
 
 Q, R = range(2)
-AL, BE, S2 = range(3)
+AL, S2, BE = range(3)
 PR, M, TQ, TR, CA, CB = range(6)
 SENT = ((0, Q), (0, R), (1, AL), (1, BE), (1, S2)) + tuple((2, f) for f in range(6))
 NF = len(SENT)
@@ -145,50 +145,54 @@
     def __init__(self, sw, ve, vx, ss, frc, par, rows):
         self.sw, self.ve, self.vx, self.ss, self.frc, self.par, self.rows = sw, ve, vx, ss, frc, par, rows
 
-    def base(self, p, lag, mod):
-        x = p * (8 * UN) - 8 * UN * lag
-        return pl.multiple_of(lax.rem(x + (lag * mod if lag else 0), mod), 8 * UN)
-
     def step(self, p, stages):
         sw, rows, unit = self.sw, self.rows, 8 * UN
         row = pl.multiple_of(p * unit, unit)
-        ss = [View(self.ss, PAD, self.base(p, lag, rows)) for lag in (0, 2, 3)]
-        par = [View(self.par, PAD, self.base(p, lag, rows)) for lag in (0, 3)]
+        turn = pl.multiple_of(lax.rem(row, rows), unit)
+        late = pl.multiple_of(lax.rem(row + rows - 4 * unit, rows), unit)
         slots = [View(self.frc, PAD, pl.multiple_of(lax.rem(p + k, 2) * unit, unit)) for k in (0, 1)]
-        was = lambda lag: View(self.ve, FRONT - lag * unit, row)
-        now = lambda lag: View(self.ve, FRONT + rows - lag * unit, row)
-        vx = View(self.vx, PAD, self.base(p, 0, 2 * rows))
-        shifted = View(self.vx, PAD, pl.multiple_of(lax.rem(row + 3 * rows - 4 * unit, 2 * rows), unit))
+        was = lambda ref, lag: View(ref, FRONT - lag * unit, row)
+        now = lambda ref, lag: View(ref, FRONT + rows - lag * unit, row)
+        par = lambda lag: View(self.par, FRONT - lag * unit, turn)
+        ve, ss = self.ve, self.ss
         todo = {
-            "velocity": (was(3), now(3), ss[2], slots[1], par[1]),
-            "force": (ss[1], slots[0]),
-            "stress": (was(0), vx, ss[0], ss[0], par[0]),
-            "spread": (now(4), shifted),
+            "velocity": (was(ve, 3), now(ve, 3), now(ss, 3), slots[1], par(3)),
+            "force": (now(ss, 2), slots[0]),
+            "stress": (was(ve, 0), View(self.vx, PAD, turn), was(ss, 0), now(ss, 0), par(0)),
+            "spread": (now(ve, 4), View(self.vx, PAD, late)),
         }
         for name in stages:
             for i in range(UN):
                 getattr(sw, name)(*todo[name], i)
 
-    def run(self):
+    def run(self, lo, hi):
+        every = ("velocity", "force", "stress", "spread")
         steps = ITERS * self.rows // (8 * UN)
-        every = ("velocity", "force", "stress", "spread")
-        parts = (
+        for a, b, stages in (
             (0, 2, every[2:3]), (2, 3, every[1:3]), (3, 4, every[:3]),
-            (4, steps, every), (steps, steps + 3, every[:2]),
-        )
-        for lo, hi, stages in parts:
+            (4, steps, every), (steps, steps + 2, every[:2]), (steps + 2, steps + 3, every[:1]),
+        ):
+            if isinstance(lo, int):
+                a, b = max(a, lo), min(b, hi)
+                if a >= b:
+                    continue
+            elif a != 4:
+                continue
+            else:
+                a, b = lo, hi
+
             def body(p, carry):
                 self.step(p, stages)
                 return carry
 
-            lax.fori_loop(lo, hi, body, 0)
+            lax.fori_loop(a, b, body, 0)
 
 
 def core_kernel(
     nx, ny, rows, cols,
     vel, stress, strength, mass, wind, current, mask, water,
     vel_out, stress_out, total_out,
-    strength_v, mass_v, mask_v, water_v, vel_v, stress_v, wind_v, current_v,
+    strength_v, mass_v, mask_v, water_v, wind_v, current_v,
     ve, vx, ss, frc, par, acc,
     pack_u, pack_d, recv_u, recv_d, own_l, own_r, recv_l, recv_r,
     corner_u, corner_d, corner_in,
@@ -205,18 +209,21 @@
     zero = jnp.zeros((8, LANE), f32)
 
     def loads(c):
-        part = pl.ds(c * per, per)
+        part = pl.ds(pl.multiple_of(c * per, 8), per)
+        later = pl.ds(pl.multiple_of(c * per + FRONT, 8), per)
         both = slice(None)
-        pairs = (
+        pairs = [
             (strength.at[part], strength_v.at[part]),
             (mass.at[part], mass_v.at[part]),
             (mask.at[part], mask_v.at[part]),
             (water.at[part], water_v.at[part]),
-            (vel.at[both, part], vel_v.at[both, part]),
-            (stress.at[both, part], stress_v.at[both, part]),
             (wind.at[both, part], wind_v.at[both, part]),
             (current.at[both, part], current_v.at[both, part]),
-        )
+        ]
+        for j in range(n):
+            tile = pl.ds(j * LANE, LANE)
+            pairs.append((vel.at[both, part, tile], ve.at[both, j, later]))
+            pairs.append((stress.at[both, part, tile], ss.at[both, j, later]))
         return [pltpu.make_async_copy(a, b, load_sem.at[c, k]) for k, (a, b) in enumerate(pairs)]
 
     for c in [0, chunks - 1] + list(range(1, chunks - 1)):
@@ -226,24 +233,25 @@
     count = nx * ny
     me = ix * ny + iy
 
-    def target(k):
-        t = lax.rem(me + k, count)
-        return (t // ny, lax.rem(t, ny))
+    def others(act):
+        def line(x, carry):
+            for y in range(ny):
+                @pl.when((x != ix) | (y != iy))
+                def _():
+                    act(x, y)
+            return carry
+
+        lax.fori_loop(0, nx, line, 0)
 
     barrier = pltpu.get_barrier_semaphore()
-
-    def greet(k, c):
-        pl.semaphore_signal(barrier, inc=1, device_id=target(k), device_id_type=MESH)
-        return c
-
-    lax.fori_loop(1, count, greet, 0)
+    others(lambda x, y: pl.semaphore_signal(barrier, inc=1, device_id=(x, y), device_id_type=MESH))
 
     for j in range(n):
         for f in range(2):
             ve[f, j, FRONT - 8 : FRONT, :] = zero
             vx[f, j, 0:8, :] = zero
         for f in range(3):
-            ss[f, j, rows + PAD : rows + 16, :] = zero
+            ss[f, j, FRONT + (ITERS + 1) * rows : FRONT + (ITERS + 1) * rows + 8, :] = zero
     for st in (row_va, row_vb, row_sa, row_sb, row_x, col_va, col_vb, col_sa, col_sb, col_x):
         for side in range(2):
             for f in range(st.shape[1]):
@@ -254,8 +262,7 @@
     sw = Sweep(n, False)
 
     def prepare(base, i):
-        rowsl, at = rows8((base, 8 * i)), rows8((base, 8 * i + PAD))
-        first = rows8((base, 8 * i + FRONT))
+        rowsl, at = rows8((base, 8 * i)), rows8((base, 8 * i + FRONT))
         ends = []
         for j in range(n):
             src = (rowsl, slice(j * LANE, (j + 1) * LANE))
@@ -267,8 +274,8 @@
             scale = (0.5 * w) / (diagonal * diagonal + turning * turning)
             tx = wind_v[(0,) + src] + drag_coef * current_v[(0,) + src]
             ty = wind_v[(1,) + src] + drag_coef * current_v[(1,) + src]
-            u, v = vel_v[(0,) + src], vel_v[(1,) + src]
-            s1, s2, s12 = (stress_v[(i,) + src] for i in range(3))
+            u, v = ve[0, j, at, :], ve[1, j, at, :]
+            s1, s2, s12 = (ss[f, j, at, :] for f in range(3))
             t = s12 + s12
             q, r = u + v, u - v
             moving = {Q: q, R: r}
@@ -282,8 +289,8 @@
                 CB: turning * scale,
             }
             for f, x in moving.items():
-                ve[f, j, first, :] = x
-            for f, x in state.items():
+                ve[f, j, at, :] = x
+            for f, x in ((AL, state[AL]), (BE, state[BE])):
                 ss[f, j, at, :] = x
             for f, x in fixed.items():
                 par[f, j, at, :] = x
@@ -298,21 +305,21 @@
         for i in range(2):
             packed[i, rowsl, :] = packs[i]
 
+    group = min(UN, per // 8)
+
     def prepare_chunk(c):
         for cp in loads(c):
             cp.wait()
 
-        group = min(UN, per // 8)
-
         def body(p, carry):
-            base = pl.multiple_of(p * (8 * group), 8 * group)
+            base = pl.multiple_of(c * per + p * (8 * group), 8 * group)
             for i in range(group):
                 prepare(base, i)
             for i in range(group):
                 sw.spread(View(ve, FRONT, base), View(vx, PAD, base), i)
             return carry
 
-        lax.fori_loop(c * (per // 8) // group, (c + 1) * (per // 8) // group, body, 0)
+        lax.fori_loop(0, per // 8 // group, body, 0)
 
     def exists(d):
         return (ix + d[0] >= 0) & (ix + d[0] < nx) & (iy + d[1] >= 0) & (iy + d[1] < ny)
@@ -341,7 +348,7 @@
 
     def plane(i, j, block):
         a, f = SENT[i]
-        row = block * 8 + (FRONT, PAD, PAD)[a]
+        row = block * 8 + FRONT
         return (ve, ss, par)[a][f, j, row : row + 8, :]
 
     prepare_chunk(0)
@@ -357,8 +364,42 @@
         def _():
             message(d, 0)[0].start()
 
-    for c in range(1, chunks - 1):
+    for i in range(NF):
+        a, f = SENT[i]
+        dst = (row_va, row_sa, row_p)[a]
+        for j in range(n):
+            x, y = (roll(plane(i, j, b), 4, 0) for b in (0, 1))
+            dst[0, f, j, 8:16, :] = x
+            dst[0, f, j, 16:24, :] = select(sub < 4, x, y)
+            x, y = (roll(plane(i, j, b), 4, 0) for b in (blocks - 2, blocks - 1))
+            dst[1, f, j, 8:16, :] = select(sub < 4, x, y)
+            dst[1, f, j, 16:24, :] = y
+
+    stream = Stream(sw, ve, vx, ss, frc, par, rows)
+    pace = per // (8 * UN)
+    begin = 1
+    if pace:
+        stream.run(0, pace)
+        while begin < chunks - 1 and begin * pace < 4:
+            prepare_chunk(begin)
+            stream.run(begin * pace, (begin + 1) * pace)
+            begin += 1
+
+    def advance(c, carry):
         prepare_chunk(c)
+        if pace:
+            stream.run(c * pace, (c + 1) * pace)
+        return carry
+
+    lax.fori_loop(begin, chunks - 1, advance, 0)
+
+    def wrap(i, carry):
+        for f in range(6):
+            for j in range(n):
+                par[f, j, rows8((8 * i, FRONT - 24 * UN)), :] = par[f, j, rows8((8 * i, FRONT + rows - 24 * UN)), :]
+        return carry
+
+    lax.fori_loop(0, 3 * UN, wrap, 0)
 
     for i in range(2):
         for t in range(tall):
@@ -388,18 +429,7 @@
         def _():
             message(d, 1)[0].start()
 
-    for i in range(NF):
-        a, f = SENT[i]
-        dst = (row_va, row_sa, row_p)[a]
-        for j in range(n):
-            x, y = (roll(plane(i, j, b), 4, 0) for b in (0, 1))
-            dst[0, f, j, 8:16, :] = x
-            dst[0, f, j, 16:24, :] = select(sub < 4, x, y)
-            x, y = (roll(plane(i, j, b), 4, 0) for b in (blocks - 2, blocks - 1))
-            dst[1, f, j, 8:16, :] = select(sub < 4, x, y)
-            dst[1, f, j, 16:24, :] = y
-
-    Stream(sw, ve, vx, ss, frc, par, rows).run()
+    stream.run((chunks - 1) * pace, ITERS * blocks // UN + 3)
 
     def clear(ref, lead):
         for i in lead:
@@ -500,12 +530,11 @@
 
         base = pl.multiple_of(p * (8 * group), 8 * group)
         for i in range(group):
-            sw.reduce(View(ve, last - rows + lead, base), View(ve, last + lead, base), View(par, PAD + lead, base), i, add)
+            sw.reduce(View(ve, last - rows + lead, base), View(ve, last + lead, base), View(par, FRONT + lead, base), i, add)
         for i, z in part.items():
             acc[i] += z
 
-    group = 2
-    lax.fori_loop(0, (blocks - 2) // group, lambda p, c: (reduce_rows(p, group, 8), c)[1], 0)
+    lax.fori_loop(0, (blocks - 2) // 2, lambda p, c: (reduce_rows(p, 2, 8), c)[1], 0)
 
     for j in range(n):
         good = lane >= 4 if j == 0 else lane < LANE - 4 if j == n - 1 else None
@@ -520,24 +549,21 @@
     part = jnp.where(half, x, y)
     mine[...] = part
 
-    def sum_copy(k):
+    def sum_copy(x, y, origin):
         return pltpu.make_async_remote_copy(
-            src_ref=mine, dst_ref=slots.at[me], send_sem=sum_send.at[k], recv_sem=sum_recv.at[k],
-            device_id=target(k), device_id_type=MESH,
+            src_ref=mine, dst_ref=slots.at[me], send_sem=sum_send.at[x * ny + y],
+            recv_sem=sum_recv.at[origin], device_id=(x, y), device_id_type=MESH,
         )
 
-    def start(k, c):
-        sum_copy(k).start()
-        return c
-
-    lax.fori_loop(1, count, start, 0)
+    others(lambda x, y: sum_copy(x, y, me).start())
     slots[pl.ds(me, 1)] = part[None]
 
     for t in range(tall):
         for o, (a, f) in enumerate(SENT[:5]):
             x = select(sub < 4, col_e[a][0, f, t, 16:24, :], col_e[a][1, f, t, 8:16, :])
-            edge_t[o * 8 : o * 8 + 8, :] = roll(x, 4, 0)
-        edge[t * LANE : (t + 1) * LANE, :] = edge_t[...].T
+            edge_t[t, o * 8 : o * 8 + 8, :] = roll(x, 4, 0)
+    for t in range(tall):
+        edge[t * LANE : (t + 1) * LANE, :] = edge_t[t].T
 
     def emit(rowsl, src):
         ev = edge[rowsl, :]
@@ -561,22 +587,22 @@
 
     emit(slice(0, 8), row_strip(0))
     emit(slice(rows - 8, rows), row_strip(1))
-    batch = 6 if (blocks - 2) % 6 == 0 else 2
+
+    def emit_rows(base, count):
+        for i in range(1, count + 1):
+            at = rows8((base, 8 * i + last))
+            emit(rows8((base, 8 * i)), [(ve, at), (ss, at)])
+
+    batch = min(10, blocks - 2)
 
     def body(p, c):
-        base = pl.multiple_of(p * (8 * batch), 8)
-        for i in range(1, batch + 1):
-            src = [(ve, rows8((base, 8 * i + last))), (ss, rows8((base, 8 * i + PAD)))]
-            emit(rows8((base, 8 * i)), src)
+        emit_rows(pl.multiple_of(p * (8 * batch), 8), batch)
         return c
 
     lax.fori_loop(0, (blocks - 2) // batch, body, 0)
-
-    def wait(k, c):
-        sum_copy(k).wait()
-        return c
-
-    lax.fori_loop(1, count, wait, 0)
+    emit_rows((blocks - 2) // batch * batch * 8, (blocks - 2) % batch)
+
+    others(lambda x, y: sum_copy(x, y, x * ny + y).wait())
     total = slots[0]
     for i in range(1, count):
         total = total + slots[i]
@@ -586,13 +612,18 @@
     total_out[...] = jnp.where(half, x, y)
 
 
-def write_kernel(vel, stress, new_vel, new_stress, sem):
+def write_kernel(vel, stress, total, new_vel, new_stress, residual, kinetic, sem):
     copies = [
-        pltpu.make_async_copy(vel, new_vel, sem.at[0]),
-        pltpu.make_async_copy(stress, new_stress, sem.at[1]),
+        pltpu.make_async_copy(a.at[f, part], b.at[f, part], sem.at[k, f, h])
+        for k, (a, b) in enumerate(((vel, new_vel), (stress, new_stress)))
+        for f in range(a.shape[0])
+        for h, part in enumerate((pl.ds(0, a.shape[1] // 2), pl.ds(a.shape[1] // 2, a.shape[1] // 2)))
     ]
     for c in copies:
         c.start()
+    x = total[...]
+    residual[0, 0] = x[0, 0]
+    kinetic[0, 0] = x[0, LANE - 1]
     for c in copies:
         c.wait()
 
@@ -613,10 +644,10 @@
         out_specs=(vmem, vmem, vmem),
         scratch_shapes=[
             V((rows, cols), f32), V((rows, cols), f32), V((rows, cols), i32), V((rows, cols), i32),
-            V((2, rows, cols), f32), V((3, rows, cols), f32), V((2, rows, cols), f32), V((2, rows, cols), f32),
-            V((2, n, FRONT + (ITERS + 1) * rows, LANE), f32), V((2, n, 2 * rows + PAD, LANE), f32),
-            V((3, n, strip, LANE), f32), V((2, n, 2 * 8 * UN + PAD, LANE), f32),
-            V((6, n, strip, LANE), f32), V((2 * n, 8, LANE), f32),
+            V((2, rows, cols), f32), V((2, rows, cols), f32),
+            V((2, n, FRONT + (ITERS + 1) * rows, LANE), f32), V((2, n, rows + PAD, LANE), f32),
+            V((3, n, FRONT + (ITERS + 1) * rows + 8, LANE), f32), V((2, n, 2 * 8 * UN + PAD, LANE), f32),
+            V((6, n, FRONT + rows, LANE), f32), V((2 * n, 8, LANE), f32),
             V((PAIRS, n, 8, LANE), f32), V((PAIRS, n, 8, LANE), f32),
             V((PAIRS, n, 8, LANE), f32), V((PAIRS, n, 8, LANE), f32),
             V((NF, tall, 8, LANE), f32), V((NF, tall, 8, LANE), f32),
@@ -628,12 +659,12 @@
             V((2, 2, tall + 1, 32, LANE), f32), V((2, 2, tall + 1, 32, LANE), f32),
             V((2, 3, tall + 1, 32, LANE), f32), V((2, 3, tall + 1, 32, LANE), f32), V((2, 2, tall + 1, 32, LANE), f32),
             V((2, 2, tall + 1, 32, LANE), f32), V((2, 6, tall + 1, 32, LANE), f32),
-            V((2, rows, LANE), f32), V((LANE, LANE), f32), V((rows, LANE), f32),
+            V((2, rows, LANE), f32), V((tall, LANE, LANE), f32), V((rows, LANE), f32),
             V((1, LANE), f32), V((count, 1, LANE), f32),
-            dma((8, 8)), dma((10,)), dma((10,)), dma((count,)), dma((count,)),
+            dma((8, 6 + 2 * n)), dma((10,)), dma((10,)), dma((count,)), dma((count,)),
         ],
         compiler_params=pltpu.CompilerParams(
-            collective_id=0, has_side_effects=True, vmem_limit_bytes=48 << 20
+            collective_id=0, has_side_effects=True, vmem_limit_bytes=57 << 20
         ),
         name="core",
     )(
@@ -642,19 +673,22 @@
             for x in (velocity, stress, strength, ice_mass, wind, current, ice_mask, open_water)
         ]
     )
-    new_vel, new_stress = pl.pallas_call(
+    smem = pl.BlockSpec(memory_space=pltpu.SMEM)
+    new_vel, new_stress, residual, kinetic = pl.pallas_call(
         write_kernel,
         out_shape=(
             jax.ShapeDtypeStruct(velocity.shape, f32),
             jax.ShapeDtypeStruct(stress.shape, f32),
+            jax.ShapeDtypeStruct((1, 1), f32),
+            jax.ShapeDtypeStruct((1, 1), f32),
         ),
-        in_specs=[vmem, vmem],
-        out_specs=(hbm, hbm),
-        scratch_shapes=[dma((2,))],
-        compiler_params=pltpu.CompilerParams(vmem_limit_bytes=8 << 20),
+        in_specs=[vmem, vmem, vmem],
+        out_specs=(hbm, hbm, smem, smem),
+        scratch_shapes=[dma((2, 3, 2))],
+        compiler_params=pltpu.CompilerParams(vmem_limit_bytes=1 << 20),
         name="write",
-    )(new_vel, new_stress)
-    return new_vel, new_stress, total[0, 0], total[0, LANE - 1]
+    )(new_vel, new_stress, total)
+    return new_vel, new_stress, residual.reshape(()), kinetic.reshape(())
 
 
 def solution(mesh):

time: 35.8 us -> 31.7 us (0.89)
  Pallas kernels: 34.4 us -> 30.9 us
  local copies, waits for them, and re-layouts: 0.58 us -> 0 us
    pallas_call x1, Pallas kernels: 32.1 us -> 27.9 us  [per_device(): pl.pallas_call(functools.partial(core_kernel, nx, ny, rows, cols), out_sh...]
    pallas_call x1, Pallas kernels: 2.37 us -> 2.96 us  [per_device(): pl.pallas_call(write_kernel, out_shape=(jax.ShapeDtypeStruct(velocity.sha...]
    slice x1 -> x0, local copies, waits for them, and re-layouts: 0.58 us -> none  [per_device(): return (new_vel, new_stress, total[0, 0], total[0, LANE - 1])]
where the time goes in v3:
time: 31.7 us; the launch traced here: 31.5 us
  Pallas kernels  30.9 us (97%)
  between operations  0.64 us (2%)
    pallas_call x1, Pallas kernels, per_device(): pl.pallas_call(functools.partial(core_kernel, nx, ny, rows, cols), out_sh...  27.9 us
    pallas_call x1, Pallas kernels, per_device(): pl.pallas_call(write_kernel, out_shape=(jax.ShapeDtypeStruct(velocity.sha...  2.96 us

profile of v3, /device:TPU:0, one launch (start us, length us, event | category | flops | bytes accessed | tf_op | source)
XLA Modules:
  0.0 31.5 jit_solution(1198893311683341270)
XLA Ops:
  0.6 27.9 %core.1 = (f32[2,512,512]{2,1,0:T(8,128)S(1)}, f32[3,512,512]{2,1,0:T(8,128)S(1)}, f32[1,128]{1,0:T(1,128)S(1)}) custom-call(f32[2,512,512]{2,1,0:T(8,128)} %vel.1, f32[3,512,512]{2,1,0:T(8,128)} %stress.1, f32[512,512]{1,0:T(8,128)} %strength.1, f32[512,512]{1,0:T(8,128)} %mass.1, f32[2,512,512]{2,1,0:T(8,128)} %wind.1, f32[2,512,512]{2,1,0:T(8,128)} %current.1, ...), custom_call_target="tpu_custom_call" | custom-call | tf_op jit(solution)/shard_map/core/pallas_call | solution.py:640
  28.6 3.0 %write.1 = (f32[2,512,512]{2,1,0:T(8,128)}, f32[3,512,512]{2,1,0:T(8,128)}, f32[1,1]{1,0:T(1,128)}, f32[1,1]{1,0:T(1,128)}) custom-call(f32[2,512,512]{2,1,0:T(8,128)S(1)} %get-tuple-element.11.vel, f32[3,512,512]{2,1,0:T(8,128)S(1)} %get-tuple-element.12.stress, f32[1,128]{1,0:T(1,128)S(1)} %get-tuple-element.13.total), custom_call_target="tpu_custom_call" | custom-call | tf_op jit(solution)/shard_map/write/pallas_call | solution.py:677

commit v4 on v3

--- a/solution.py
+++ b/solution.py
@@ -198,7 +198,7 @@
     corner_u, corner_d, corner_in,
     row_va, row_vb, row_sa, row_sb, row_x, row_f, row_p, col_va, col_vb, col_sa, col_sb, col_x, col_f, col_p,
     packed, edge_t, edge, mine, slots,
-    load_sem, send_sem, recv_sem, sum_send, sum_recv,
+    load_sem, send_sem, recv_sem, sum_sem,
 ):
     ix = lax.axis_index("gx")
     iy = lax.axis_index("gy")
@@ -234,8 +234,11 @@
     me = ix * ny + iy
 
     def others(act):
-        def line(x, carry):
-            for y in range(ny):
+        def line(k, carry):
+            x = lax.rem(ix + nx // 2 + k, nx)
+            for m in range(ny):
+                y = lax.rem(iy + ny // 2 + m, ny)
+
                 @pl.when((x != ix) | (y != iy))
                 def _():
                     act(x, y)
@@ -305,7 +308,7 @@
         for i in range(2):
             packed[i, rowsl, :] = packs[i]
 
-    group = min(UN, per // 8)
+    group = min(8, per // 8)
 
     def prepare_chunk(c):
         for cp in loads(c):
@@ -549,13 +552,13 @@
     part = jnp.where(half, x, y)
     mine[...] = part
 
-    def sum_copy(x, y, origin):
+    def sum_copy(x, y):
         return pltpu.make_async_remote_copy(
-            src_ref=mine, dst_ref=slots.at[me], send_sem=sum_send.at[x * ny + y],
-            recv_sem=sum_recv.at[origin], device_id=(x, y), device_id_type=MESH,
+            src_ref=mine, dst_ref=slots.at[me], send_sem=sum_sem.at[0], recv_sem=sum_sem.at[1],
+            device_id=(x, y), device_id_type=MESH,
         )
 
-    others(lambda x, y: sum_copy(x, y, me).start())
+    others(lambda x, y: sum_copy(x, y).start())
     slots[pl.ds(me, 1)] = part[None]
 
     for t in range(tall):
@@ -602,17 +605,20 @@
     lax.fori_loop(0, (blocks - 2) // batch, body, 0)
     emit_rows((blocks - 2) // batch * batch * 8, (blocks - 2) % batch)
 
-    others(lambda x, y: sum_copy(x, y, x * ny + y).wait())
-    total = slots[0]
-    for i in range(1, count):
-        total = total + slots[i]
+    for i in range(2):
+        most = slots.at[pl.ds(0, count - 1)]
+        pltpu.make_async_copy(most, most, sum_sem.at[i]).wait()
+    total = [slots[i] for i in range(count)]
+    while len(total) > 1:
+        total = [a + b for a, b in zip(total[::2], total[1::2])] + total[len(total) // 2 * 2 :]
+    total = total[0]
     scale = 1.0 / (rows * nx * cols * ny)
     x = jnp.sum(jnp.where(half, total, 0.0), axis=1, keepdims=True) * (0.5 * scale)
     y = jnp.sum(jnp.where(half, 0.0, total), axis=1, keepdims=True) * (0.0625 * scale)
     total_out[...] = jnp.where(half, x, y)
 
 
-def write_kernel(vel, stress, total, new_vel, new_stress, residual, kinetic, sem):
+def write_kernel(vel, stress, total, new_vel, new_stress, residual, kinetic, res, kin, sem, few):
     copies = [
         pltpu.make_async_copy(a.at[f, part], b.at[f, part], sem.at[k, f, h])
         for k, (a, b) in enumerate(((vel, new_vel), (stress, new_stress)))
@@ -622,8 +628,11 @@
     for c in copies:
         c.start()
     x = total[...]
-    residual[0, 0] = x[0, 0]
-    kinetic[0, 0] = x[0, LANE - 1]
+    res[0, 0] = x[0, 0]
+    kin[0, 0] = x[0, LANE - 1]
+    for i, (a, b) in enumerate(((res, residual), (kin, kinetic))):
+        copies.append(pltpu.make_async_copy(a, b, few.at[i]))
+        copies[-1].start()
     for c in copies:
         c.wait()
 
@@ -645,9 +654,9 @@
         scratch_shapes=[
             V((rows, cols), f32), V((rows, cols), f32), V((rows, cols), i32), V((rows, cols), i32),
             V((2, rows, cols), f32), V((2, rows, cols), f32),
-            V((2, n, FRONT + (ITERS + 1) * rows, LANE), f32), V((2, n, rows + PAD, LANE), f32),
+            V((2, n, FRONT + (ITERS + 1) * rows + 8, LANE), f32), V((2, n, rows + PAD, LANE), f32),
             V((3, n, FRONT + (ITERS + 1) * rows + 8, LANE), f32), V((2, n, 2 * 8 * UN + PAD, LANE), f32),
-            V((6, n, FRONT + rows, LANE), f32), V((2 * n, 8, LANE), f32),
+            V((6, n, FRONT + rows + 8, LANE), f32), V((2 * n, 8, LANE), f32),
             V((PAIRS, n, 8, LANE), f32), V((PAIRS, n, 8, LANE), f32),
             V((PAIRS, n, 8, LANE), f32), V((PAIRS, n, 8, LANE), f32),
             V((NF, tall, 8, LANE), f32), V((NF, tall, 8, LANE), f32),
@@ -661,7 +670,7 @@
             V((2, 2, tall + 1, 32, LANE), f32), V((2, 6, tall + 1, 32, LANE), f32),
             V((2, rows, LANE), f32), V((tall, LANE, LANE), f32), V((rows, LANE), f32),
             V((1, LANE), f32), V((count, 1, LANE), f32),
-            dma((8, 6 + 2 * n)), dma((10,)), dma((10,)), dma((count,)), dma((count,)),
+            dma((8, 6 + 2 * n)), dma((10,)), dma((10,)), dma((2,)),
         ],
         compiler_params=pltpu.CompilerParams(
             collective_id=0, has_side_effects=True, vmem_limit_bytes=57 << 20
@@ -673,7 +682,6 @@
             for x in (velocity, stress, strength, ice_mass, wind, current, ice_mask, open_water)
         ]
     )
-    smem = pl.BlockSpec(memory_space=pltpu.SMEM)
     new_vel, new_stress, residual, kinetic = pl.pallas_call(
         write_kernel,
         out_shape=(
@@ -683,8 +691,8 @@
             jax.ShapeDtypeStruct((1, 1), f32),
         ),
         in_specs=[vmem, vmem, vmem],
-        out_specs=(hbm, hbm, smem, smem),
-        scratch_shapes=[dma((2, 3, 2))],
+        out_specs=(hbm,) * 4,
+        scratch_shapes=[pltpu.SMEM((1, 1), f32), pltpu.SMEM((1, 1), f32), dma((2, 3, 2)), dma((2,))],
         compiler_params=pltpu.CompilerParams(vmem_limit_bytes=1 << 20),
         name="write",
     )(new_vel, new_stress, total)

time: 31.7 us -> 30.1 us (0.950)
  Pallas kernels: 30.9 us -> 29.3 us
    pallas_call x1, Pallas kernels: 27.9 us -> 26.8 us  [per_device(): pl.pallas_call(functools.partial(core_kernel, nx, ny, rows, cols), out_sh...]
    pallas_call x1, Pallas kernels: 2.96 us -> 2.47 us  [per_device(): pl.pallas_call(write_kernel, out_shape=(jax.ShapeDtypeStruct(velocity.sha...]
where the time goes in v4:
time: 30.1 us; the launch traced here: 29.9 us
  Pallas kernels  29.3 us (97%)
  between operations  0.64 us (2%)
    pallas_call x1, Pallas kernels, per_device(): pl.pallas_call(functools.partial(core_kernel, nx, ny, rows, cols), out_sh...  26.8 us
    pallas_call x1, Pallas kernels, per_device(): pl.pallas_call(write_kernel, out_shape=(jax.ShapeDtypeStruct(velocity.sha...  2.47 us

profile of v4, /device:TPU:0, one launch (start us, length us, event | category | flops | bytes accessed | tf_op | source)
XLA Modules:
  0.0 29.9 jit_solution(17817728747361569851)
XLA Ops:
  0.6 26.8 %core.1 = (f32[2,512,512]{2,1,0:T(8,128)S(1)}, f32[3,512,512]{2,1,0:T(8,128)S(1)}, f32[1,128]{1,0:T(1,128)S(1)}) custom-call(f32[2,512,512]{2,1,0:T(8,128)} %vel.1, f32[3,512,512]{2,1,0:T(8,128)} %stress.1, f32[512,512]{1,0:T(8,128)} %strength.1, f32[512,512]{1,0:T(8,128)} %mass.1, f32[2,512,512]{2,1,0:T(8,128)} %wind.1, f32[2,512,512]{2,1,0:T(8,128)} %current.1, ...), custom_call_target="tpu_custom_call" | custom-call | tf_op jit(solution)/shard_map/core/pallas_call | solution.py:649
  27.4 2.5 %write.1 = (f32[2,512,512]{2,1,0:T(8,128)}, f32[3,512,512]{2,1,0:T(8,128)}, f32[1,1]{1,0:T(1,128)}, f32[1,1]{1,0:T(1,128)}) custom-call(f32[2,512,512]{2,1,0:T(8,128)S(1)} %get-tuple-element.11.vel, f32[3,512,512]{2,1,0:T(8,128)S(1)} %get-tuple-element.12.stress, f32[1,128]{1,0:T(1,128)S(1)} %get-tuple-element.13.total), custom_call_target="tpu_custom_call" | custom-call | tf_op jit(solution)/shard_map/write/pallas_call | solution.py:685

commit v5 on v4

--- a/solution.py
+++ b/solution.py
@@ -224,7 +224,7 @@
             tile = pl.ds(j * LANE, LANE)
             pairs.append((vel.at[both, part, tile], ve.at[both, j, later]))
             pairs.append((stress.at[both, part, tile], ss.at[both, j, later]))
-        return [pltpu.make_async_copy(a, b, load_sem.at[c, k]) for k, (a, b) in enumerate(pairs)]
+        return [pltpu.make_async_copy(a, b, load_sem.at[c]) for a, b in pairs]
 
     for c in [0, chunks - 1] + list(range(1, chunks - 1)):
         for cp in loads(c):
@@ -311,8 +311,8 @@
     group = min(8, per // 8)
 
     def prepare_chunk(c):
-        for cp in loads(c):
-            cp.wait()
+        size = ve.at[0, :, pl.ds(0, 13 * per)]
+        pltpu.make_async_copy(size, size, load_sem.at[c]).wait()
 
         def body(p, carry):
             base = pl.multiple_of(c * per + p * (8 * group), 8 * group)
@@ -620,19 +620,20 @@
 
 def write_kernel(vel, stress, total, new_vel, new_stress, residual, kinetic, res, kin, sem, few):
     copies = [
-        pltpu.make_async_copy(a.at[f, part], b.at[f, part], sem.at[k, f, h])
+        pltpu.make_async_copy(a.at[f, part], b.at[f, part], sem.at[k])
         for k, (a, b) in enumerate(((vel, new_vel), (stress, new_stress)))
         for f in range(a.shape[0])
-        for h, part in enumerate((pl.ds(0, a.shape[1] // 2), pl.ds(a.shape[1] // 2, a.shape[1] // 2)))
+        for part in (pl.ds(0, a.shape[1] // 2), pl.ds(a.shape[1] // 2, a.shape[1] // 2))
     ]
     for c in copies:
         c.start()
     x = total[...]
     res[0, 0] = x[0, 0]
     kin[0, 0] = x[0, LANE - 1]
-    for i, (a, b) in enumerate(((res, residual), (kin, kinetic))):
-        copies.append(pltpu.make_async_copy(a, b, few.at[i]))
-        copies[-1].start()
+    copies = [pltpu.make_async_copy(a, b, few.at[i]) for i, (a, b) in enumerate(((res, residual), (kin, kinetic)))]
+    for c in copies:
+        c.start()
+    copies += [pltpu.make_async_copy(a, b, sem.at[k]) for k, (a, b) in enumerate(((vel, new_vel), (stress, new_stress)))]
     for c in copies:
         c.wait()
 
@@ -670,7 +671,7 @@
             V((2, 2, tall + 1, 32, LANE), f32), V((2, 6, tall + 1, 32, LANE), f32),
             V((2, rows, LANE), f32), V((tall, LANE, LANE), f32), V((rows, LANE), f32),
             V((1, LANE), f32), V((count, 1, LANE), f32),
-            dma((8, 6 + 2 * n)), dma((10,)), dma((10,)), dma((2,)),
+            dma((8,)), dma((10,)), dma((10,)), dma((2,)),
         ],
         compiler_params=pltpu.CompilerParams(
             collective_id=0, has_side_effects=True, vmem_limit_bytes=57 << 20
@@ -692,7 +693,7 @@
         ),
         in_specs=[vmem, vmem, vmem],
         out_specs=(hbm,) * 4,
-        scratch_shapes=[pltpu.SMEM((1, 1), f32), pltpu.SMEM((1, 1), f32), dma((2, 3, 2)), dma((2,))],
+        scratch_shapes=[pltpu.SMEM((1, 1), f32), pltpu.SMEM((1, 1), f32), dma((2,)), dma((2,))],
         compiler_params=pltpu.CompilerParams(vmem_limit_bytes=1 << 20),
         name="write",
     )(new_vel, new_stress, total)

time: 30.1 us -> 28.9 us (0.960)
  Pallas kernels: 29.3 us -> 28.2 us
    pallas_call x1, Pallas kernels: 26.8 us -> 25.8 us  [per_device(): pl.pallas_call(functools.partial(core_kernel, nx, ny, rows, cols), out_sh...]
where the time goes in v5:
time: 28.9 us; the launch traced here: 28.8 us
  Pallas kernels  28.2 us (98%)
  between operations  0.64 us (2%)
    pallas_call x1, Pallas kernels, per_device(): pl.pallas_call(functools.partial(core_kernel, nx, ny, rows, cols), out_sh...  25.8 us
    pallas_call x1, Pallas kernels, per_device(): pl.pallas_call(write_kernel, out_shape=(jax.ShapeDtypeStruct(velocity.sha...  2.37 us

profile of v5, /device:TPU:0, one launch (start us, length us, event | category | flops | bytes accessed | tf_op | source)
XLA Modules:
  0.0 28.8 jit_solution(8340357580394514007)
XLA Ops:
  0.6 25.8 %core.1 = (f32[2,512,512]{2,1,0:T(8,128)S(1)}, f32[3,512,512]{2,1,0:T(8,128)S(1)}, f32[1,128]{1,0:T(1,128)S(1)}) custom-call(f32[2,512,512]{2,1,0:T(8,128)} %vel.1, f32[3,512,512]{2,1,0:T(8,128)} %stress.1, f32[512,512]{1,0:T(8,128)} %strength.1, f32[512,512]{1,0:T(8,128)} %mass.1, f32[2,512,512]{2,1,0:T(8,128)} %wind.1, f32[2,512,512]{2,1,0:T(8,128)} %current.1, ...), custom_call_target="tpu_custom_call" | custom-call | tf_op jit(solution)/shard_map/core/pallas_call | solution.py:650
  26.4 2.4 %write.1 = (f32[2,512,512]{2,1,0:T(8,128)}, f32[3,512,512]{2,1,0:T(8,128)}, f32[1,1]{1,0:T(1,128)}, f32[1,1]{1,0:T(1,128)}) custom-call(f32[2,512,512]{2,1,0:T(8,128)S(1)} %get-tuple-element.11.vel, f32[3,512,512]{2,1,0:T(8,128)S(1)} %get-tuple-element.12.stress, f32[1,128]{1,0:T(1,128)S(1)} %get-tuple-element.13.total), custom_call_target="tpu_custom_call" | custom-call | tf_op jit(solution)/shard_map/write/pallas_call | solution.py:686

commit v6 on v5

--- a/solution.py
+++ b/solution.py
@@ -226,7 +226,7 @@
             pairs.append((stress.at[both, part, tile], ss.at[both, j, later]))
         return [pltpu.make_async_copy(a, b, load_sem.at[c]) for a, b in pairs]
 
-    for c in [0, chunks - 1] + list(range(1, chunks - 1)):
+    for c in range(chunks):
         for cp in loads(c):
             cp.start()
 
@@ -234,17 +234,12 @@
     me = ix * ny + iy
 
     def others(act):
-        def line(k, carry):
-            x = lax.rem(ix + nx // 2 + k, nx)
-            for m in range(ny):
-                y = lax.rem(iy + ny // 2 + m, ny)
-
-                @pl.when((x != ix) | (y != iy))
-                def _():
+        xs = [lax.rem(ix + nx // 2 + k, nx) for k in range(nx)]
+        ys = [lax.rem(iy + ny // 2 + k, ny) for k in range(ny)]
+        for i, x in enumerate(xs):
+            for j, y in enumerate(ys):
+                if (nx // 2 + i) % nx or (ny // 2 + j) % ny:
                     act(x, y)
-            return carry
-
-        lax.fori_loop(0, nx, line, 0)
 
     barrier = pltpu.get_barrier_semaphore()
     others(lambda x, y: pl.semaphore_signal(barrier, inc=1, device_id=(x, y), device_id_type=MESH))
@@ -354,18 +349,38 @@
         row = block * 8 + FRONT
         return (ve, ss, par)[a][f, j, row : row + 8, :]
 
+    stream = Stream(sw, ve, vx, ss, frc, par, rows)
+    pace = per // (8 * UN)
+    begin = 1
     prepare_chunk(0)
-    prepare_chunk(chunks - 1)
+    if pace:
+        stream.run(0, pace)
+        while begin < chunks and begin * pace < 4:
+            prepare_chunk(begin)
+            stream.run(begin * pace, (begin + 1) * pace)
+            begin += 1
+
+    def advance(c, carry):
+        prepare_chunk(c)
+        if pace:
+            stream.run(c * pace, (c + 1) * pace)
+        return carry
+
+    lax.fori_loop(begin, chunks, advance, 0)
+
+    def wrap(i, carry):
+        for f in range(6):
+            for j in range(n):
+                par[f, j, rows8((8 * i, FRONT - 24 * UN)), :] = par[f, j, rows8((8 * i, FRONT + rows - 24 * UN)), :]
+        return carry
+
+    lax.fori_loop(0, 3 * UN, wrap, 0)
+
     for g in range(PAIRS):
         i0, i1 = 2 * g, min(2 * g + 1, NF - 1)
         for j in range(n):
             pack_u[g, j] = select(sub < 4, plane(i0, j, 0), roll(plane(i1, j, 0), 4, 0))
             pack_d[g, j] = select(sub < 4, roll(plane(i0, j, blocks - 1), 4, 0), plane(i1, j, blocks - 1))
-    pl.semaphore_wait(barrier, count - 1)
-    for d in DIRS[:2]:
-        @pl.when(exists(d))
-        def _():
-            message(d, 0)[0].start()
 
     for i in range(NF):
         a, f = SENT[i]
@@ -378,31 +393,11 @@
             dst[1, f, j, 8:16, :] = select(sub < 4, x, y)
             dst[1, f, j, 16:24, :] = y
 
-    stream = Stream(sw, ve, vx, ss, frc, par, rows)
-    pace = per // (8 * UN)
-    begin = 1
-    if pace:
-        stream.run(0, pace)
-        while begin < chunks - 1 and begin * pace < 4:
-            prepare_chunk(begin)
-            stream.run(begin * pace, (begin + 1) * pace)
-            begin += 1
-
-    def advance(c, carry):
-        prepare_chunk(c)
-        if pace:
-            stream.run(c * pace, (c + 1) * pace)
-        return carry
-
-    lax.fori_loop(begin, chunks - 1, advance, 0)
-
-    def wrap(i, carry):
-        for f in range(6):
-            for j in range(n):
-                par[f, j, rows8((8 * i, FRONT - 24 * UN)), :] = par[f, j, rows8((8 * i, FRONT + rows - 24 * UN)), :]
-        return carry
-
-    lax.fori_loop(0, 3 * UN, wrap, 0)
+    pl.semaphore_wait(barrier, count - 1)
+    for d in DIRS[:2]:
+        @pl.when(exists(d))
+        def _():
+            message(d, 0)[0].start()
 
     for i in range(2):
         for t in range(tall):
@@ -432,7 +427,25 @@
         def _():
             message(d, 1)[0].start()
 
-    stream.run((chunks - 1) * pace, ITERS * blocks // UN + 3)
+    stream.run(chunks * pace, ITERS * blocks // UN + 3)
+
+    last = FRONT + ITERS * rows
+    acc[...] = jnp.zeros_like(acc)
+
+    def reduce_rows(p, group, lead):
+        part = {}
+
+        def add(j, x, y):
+            for i, z in ((2 * j, x), (2 * j + 1, y)):
+                part[i] = part[i] + z if i in part else z
+
+        base = pl.multiple_of(p * (8 * group), 8 * group)
+        for i in range(group):
+            sw.reduce(View(ve, last - rows + lead, base), View(ve, last + lead, base), View(par, FRONT + lead, base), i, add)
+        for i, z in part.items():
+            acc[i] += z
+
+    lax.fori_loop(0, (blocks - 2) // 2, lambda p, c: (reduce_rows(p, 2, 8), c)[1], 0)
 
     def clear(ref, lead):
         for i in lead:
@@ -520,24 +533,6 @@
                 box[1] += select(good, y, zero)
 
             s.reduce(vb, va, p, k, add)
-
-    last = FRONT + ITERS * rows
-    acc[...] = jnp.zeros_like(acc)
-
-    def reduce_rows(p, group, lead):
-        part = {}
-
-        def add(j, x, y):
-            for i, z in ((2 * j, x), (2 * j + 1, y)):
-                part[i] = part[i] + z if i in part else z
-
-        base = pl.multiple_of(p * (8 * group), 8 * group)
-        for i in range(group):
-            sw.reduce(View(ve, last - rows + lead, base), View(ve, last + lead, base), View(par, FRONT + lead, base), i, add)
-        for i, z in part.items():
-            acc[i] += z
-
-    lax.fori_loop(0, (blocks - 2) // 2, lambda p, c: (reduce_rows(p, 2, 8), c)[1], 0)
 
     for j in range(n):
         good = lane >= 4 if j == 0 else lane < LANE - 4 if j == n - 1 else None

time: 28.9 us -> 28.6 us (0.990)
  Pallas kernels: 28.2 us -> 27.9 us
    pallas_call x1, Pallas kernels: 25.8 us -> 25.5 us  [per_device(): pl.pallas_call(functools.partial(core_kernel, nx, ny, rows, cols), out_sh...]
where the time goes in v6:
time: 28.6 us; the launch traced here: 28.5 us
  Pallas kernels  27.9 us (98%)
  between operations  0.64 us (2%)
    pallas_call x1, Pallas kernels, per_device(): pl.pallas_call(functools.partial(core_kernel, nx, ny, rows, cols), out_sh...  25.5 us
    pallas_call x1, Pallas kernels, per_device(): pl.pallas_call(write_kernel, out_shape=(jax.ShapeDtypeStruct(velocity.sha...  2.37 us

profile of v6, /device:TPU:0, one launch (start us, length us, event | category | flops | bytes accessed | tf_op | source)
XLA Modules:
  0.0 28.5 jit_solution(16483020138927914452)
XLA Ops:
  0.6 25.5 %core.1 = (f32[2,512,512]{2,1,0:T(8,128)S(1)}, f32[3,512,512]{2,1,0:T(8,128)S(1)}, f32[1,128]{1,0:T(1,128)S(1)}) custom-call(f32[2,512,512]{2,1,0:T(8,128)} %vel.1, f32[3,512,512]{2,1,0:T(8,128)} %stress.1, f32[512,512]{1,0:T(8,128)} %strength.1, f32[512,512]{1,0:T(8,128)} %mass.1, f32[2,512,512]{2,1,0:T(8,128)} %wind.1, f32[2,512,512]{2,1,0:T(8,128)} %current.1, ...), custom_call_target="tpu_custom_call" | custom-call | tf_op jit(solution)/shard_map/core/pallas_call | solution.py:645
  26.1 2.4 %write.1 = (f32[2,512,512]{2,1,0:T(8,128)}, f32[3,512,512]{2,1,0:T(8,128)}, f32[1,1]{1,0:T(1,128)}, f32[1,1]{1,0:T(1,128)}) custom-call(f32[2,512,512]{2,1,0:T(8,128)S(1)} %get-tuple-element.11.vel, f32[3,512,512]{2,1,0:T(8,128)S(1)} %get-tuple-element.12.stress, f32[1,128]{1,0:T(1,128)S(1)} %get-tuple-element.13.total), custom_call_target="tpu_custom_call" | custom-call | tf_op jit(solution)/shard_map/write/pallas_call | solution.py:681
